TPU v7x, 512 devices: a whole 4x4x16 slice. The times are simulated.
512 devices in a mesh: patch: 512 (over y, x, z, core).
Axes of the slice: x: 4, y: 4, z: 16, core: 2. Of those that a mesh axis runs over, the one named last changes fastest.
Arguments:
- fields: float32 [4, 32, 32, 65536], P(None, None, None, 'patch'), may hold values from -1.5 to 4, as said below
- patch_level: int32 [65536], P('patch'), may hold values from 4 to 6
- relation: int32 [65536, 4], P('patch'), may hold values from 0 to 3
- face_half: int32 [65536, 4], P('patch'), may hold values from 0 to 1
- neighbour: int32 [65536, 4, 2], P('patch'), may hold values from 0 to 255, as said below
- send_list: int32 [512, 16, 8], P('patch'), may hold values from 0 to 127, as said below
Outputs:
- advanced: float32 [4, 32, 32, 65536], P(None, None, None, 'patch')
- time_step: float32 [], replicated
Inputs may be any that keep to these rules, and one draw needn't show every extreme that they name: `send_list`: within each device's block for one curve distance the 8 entries are distinct local patches. `neighbour`: A reference of 128 or more names a slot of a device that exists on the curve. The second reference of a face is used only where relation is 3. `fields`: h lies in [2, 4], |hu| and |hv| at most 1.5, hc in [0, h].
All inputs are finite; a program needn't handle non-finite values.
Results may differ from a plain program's by a relative error of at most 0.0003.
Values sent between devices are 32-bit elements; how exact they have to be, the bound alone decides.
No kernel may reach another device: no remote copies, remote signals or barrier semaphores. Data moves between devices by JAX's collectives and lax.ppermute only.
A program may use at most 128 MiB of HBM per device.

v0:
```python
import jax
import jax.numpy as jnp
from jax import lax
from jax.sharding import Mesh
from jax.sharding import PartitionSpec as P

HOPS = 8
NOFF = 16
PATCH = ("patch_0", "patch_1", "patch_2", "patch_3")


courant = 0.4
finest_level = 6.0


def from_behind(array, axis, by):
    devices = lax.axis_size(axis)
    pairs = [(i, i + by) for i in range(devices) if 0 <= i + by < devices]
    return lax.ppermute(array, axis, pairs)


def one_axis_at_a_time(array, axes):
    for axis in axes:
        array = lax.pmin(array, axis)
    return array


def face_strips(state):
    west_side = state[:, 0:4]
    east_side = state[:, ::-1][:, 0:4]
    south_side = jnp.swapaxes(state[:, :, 0:4], 1, 2)
    north_side = jnp.swapaxes(state[:, :, ::-1][:, :, 0:4], 1, 2)
    stacked = jnp.stack([west_side, east_side, south_side, north_side])
    return jnp.transpose(stacked, (4, 0, 1, 2, 3))


def restrict(strip):
    total = strip[..., 0::2, 0::2] + strip[..., 1::2, 0::2]
    total = total + strip[..., 0::2, 1::2]
    total = total + strip[..., 1::2, 1::2]
    return 0.25 * total


def cell_speed(state):
    depth = state[0]
    return jnp.maximum(jnp.abs(state[1] / depth), jnp.abs(state[2] / depth)) + jnp.sqrt(depth)


def fill_ghosts(near, coarse, own_near, relation, face_half):
    cells = near.shape[-1]
    middle = cells // 2
    same_level = near[:, :, 0]
    column = near[:, :, 0, :, 0, :]
    padded = jnp.concatenate([column[..., :1], column, column[..., -1:]], axis=-1)
    slope = padded[..., 2:] - padded[..., :-2]
    upper_half = (face_half == 1)[:, :, None, None]
    base_value = jnp.where(upper_half, column[..., middle:], column[..., :middle])
    base_slope = jnp.where(upper_half, slope[..., middle:], slope[..., :middle])
    base_value = jnp.repeat(base_value, 2, axis=-1)
    base_slope = jnp.repeat(base_slope, 2, axis=-1)
    weights = jnp.where(jnp.arange(cells) % 2 == 1, 0.125, -0.125).astype(near.dtype)
    interpolated = base_value + weights * base_slope
    coarser = jnp.broadcast_to(interpolated[:, :, :, None, :], same_level.shape)
    finer_ghost = jnp.concatenate([coarse[:, :, 0], coarse[:, :, 1]], axis=-1)
    mirror_sign = jnp.array(
        [
            [1.0, -1.0, 1.0, 1.0],
            [1.0, -1.0, 1.0, 1.0],
            [1.0, 1.0, -1.0, 1.0],
            [1.0, 1.0, -1.0, 1.0],
        ],
        near.dtype,
    )
    mirror = own_near * mirror_sign[None, :, :, None, None]
    choose = relation[:, :, None, None, None]
    return jnp.where(
        choose == 0,
        mirror,
        jnp.where(choose == 1, same_level, jnp.where(choose == 2, coarser, finer_ghost)),
    )


def physical(state, normal):
    depth = state[0]
    velocity = state[normal] / depth
    components = [state[normal], state[1] * velocity, state[2] * velocity, state[3] * velocity]
    components[normal] = components[normal] + 0.5 * depth * depth
    return (jnp.stack(components), jnp.abs(velocity) + jnp.sqrt(depth))


def flux_change(padded, normal):
    centre = padded[:, 1:-1]
    slope = 0.5 * (padded[:, 2:] - padded[:, :-2])
    left_state = (centre + 0.5 * slope)[:, :-1]
    right_state = (centre - 0.5 * slope)[:, 1:]
    left_flux, left_speed = physical(left_state, normal)
    right_flux, right_speed = physical(right_state, normal)
    widest = jnp.maximum(left_speed, right_speed)
    numeric_flux = 0.5 * (left_flux + right_flux) - 0.5 * widest * (right_state - left_state)
    return numeric_flux[:, 1:] - numeric_flux[:, :-1]


def advance(state, ghosts, step_ratio):
    sides = jnp.transpose(ghosts, (1, 2, 3, 4, 0))
    along_x = jnp.concatenate([sides[0][:, ::-1], state, sides[1]], axis=1)
    along_y = jnp.concatenate([sides[2][:, ::-1], jnp.swapaxes(state, 1, 2), sides[3]], axis=1)
    change = flux_change(along_x, 1) + jnp.swapaxes(flux_change(along_y, 2), 1, 2)
    return state - step_ratio * change


def hop_blocks(outgoing):
    received = [None] * NOFF
    for towards in (1, -1):
        base_slot = 0 if towards == 1 else HOPS
        blocks = [outgoing[base_slot + distance] for distance in range(HOPS)]
        for section_bit in range(HOPS.bit_length()):
            moving = [distance for distance in range(1, HOPS + 1) if distance >> section_bit & 1]
            stacked = jnp.stack([blocks[distance - 1] for distance in moving])
            arrived = from_behind(stacked, PATCH, towards * (1 << section_bit))
            for position, distance in enumerate(moving):
                blocks[distance - 1] = arrived[position]
        for distance in range(HOPS):
            received[base_slot + distance] = blocks[distance]
    return received


def on_device(fields, patch_level, relation, face_half, neighbour, send_list):
    nfields = fields.shape[0]
    cells = fields.shape[1]
    patches = fields.shape[3]
    spacing = jnp.exp2(finest_level - patch_level.astype(jnp.float32))
    top_speed = jnp.max(cell_speed(fields), axis=(0, 1))
    time_step = courant * one_axis_at_a_time(jnp.min(spacing / top_speed), PATCH)
    step_ratio = time_step / spacing
    strips = face_strips(fields)
    near_part = strips[..., 0:2, :].reshape(patches, 4, nfields, 2 * cells)
    coarse_part = restrict(strips).reshape(patches, 4, nfields, cells)
    own_pack = jnp.concatenate([near_part, coarse_part], axis=-1).reshape(patches, -1)
    outgoing = own_pack[send_list[0]]
    received = hop_blocks(outgoing)
    ghost_pool = jnp.concatenate([own_pack] + received, axis=0)
    opposite = jnp.array([1, 0, 3, 2], jnp.int32)[None, :, None]
    picked = ghost_pool.reshape(ghost_pool.shape[0], 4, -1)[neighbour, opposite]
    whole = picked.reshape(patches, 4, 2, nfields, 3 * cells)
    near = whole[..., : 2 * cells].reshape(patches, 4, 2, nfields, 2, cells)
    coarse = whole[..., 2 * cells :].reshape(patches, 4, 2, nfields, 2, cells // 2)
    ghosts = fill_ghosts(near, coarse, strips[..., 0:2, :], relation, face_half)
    return (advance(fields, ghosts, step_ratio), time_step)


def solution(mesh):
    split = Mesh(mesh.devices.reshape(4, 4, 16, 2), ("patch_0", "patch_1", "patch_2", "patch_3"))
    return jax.shard_map(
        on_device,
        mesh=split,
        in_specs=(
            P(None, None, None, PATCH),
            P(PATCH),
            P(PATCH, None),
            P(PATCH, None),
            P(PATCH, None, None),
            P(PATCH, None, None),
        ),
        out_specs=(P(None, None, None, PATCH), P()),
        check_vma=False,
    )
```

profile of v0, /device:TPU:41, one launch (start us, length us, event | category | flops | bytes accessed | tf_op | source)
XLA Modules:
  0.0 200.5 jit_solution(4860751660609337214)
XLA Ops:
  0.6 3.0 %copy.33 = f32[4,32,32,128]{3,1,2,0:T(8,128)S(1)} copy(f32[4,32,32,128]{3,2,1,0:T(8,128)} %param.8) | data formatting | bytes 4194304 | tf_op args[0]
  3.7 1.3 copy-done.2
  5.2 0.7 slice.337
  5.9 9.6 %slice.338 = f32[128,4,4,2,16]{0,4,3,2,1:T(8,128)} slice(f32[128,4,4,4,32]{0,4,3,2,1:T(8,128)S(1)} %maximum_bitcast_fusion), slice={[0:128:1], [0:4:1], [0:4:1], [1:4:2], [0:32:2]} | slice | bytes 524288 | tf_op jit(solution)/shard_map/slice | solution.py:38
  15.5 9.6 %slice.339 = f32[128,4,4,2,16]{0,4,3,2,1:T(8,128)} slice(f32[128,4,4,4,32]{0,4,3,2,1:T(8,128)S(1)} %maximum_bitcast_fusion), slice={[0:128:1], [0:4:1], [0:4:1], [0:4:2], [1:32:2]} | slice | bytes 524288 | tf_op jit(solution)/shard_map/slice | solution.py:39
  25.1 9.6 %slice.340 = f32[128,4,4,2,16]{0,4,3,2,1:T(8,128)} slice(f32[128,4,4,4,32]{0,4,3,2,1:T(8,128)S(1)} %maximum_bitcast_fusion), slice={[0:128:1], [0:4:1], [0:4:1], [1:4:2], [1:32:2]} | slice | bytes 524288 | tf_op jit(solution)/shard_map/slice | solution.py:40
  34.8 1.2 add_multiply_fusion
  36.0 0.9 pad_maximum_fusion.4
  36.9 1.4 copy.36
  38.5 1.7 gather_fusion
  40.3 1.3 slice_bitcast_fusion.10
  41.5 0.7 pad_maximum_fusion.10
  42.2 2.7 %collective-permute-start.4 = (f32[4,8,1536]{2,1,0:T(8,128)}, f32[4,8,1536]{2,1,0:T(8,128)}, u32[]{:S(2)}, u32[]{:S(2)}) collective-permute-start(f32[4,8,1536]{2,1,0:T(8,128)} %pad_maximum_fusion.10), channel_id=1, source_target_pairs={{1,0},{2,1},{3,2},{4,3},{5,4},{6,5},{7,6},{8,7},{9,8},{10,9},{11,1... | collective-permute-start | bytes 589832 | tf_op jit(solution)/shard_map/ppermute | solution.py:19
  44.9 0.7 pad_maximum_fusion.7
  45.6 3.4 %collective-permute-start = (f32[4,8,1536]{2,1,0:T(8,128)}, f32[4,8,1536]{2,1,0:T(8,128)S(1)}, u32[]{:S(2)}, u32[]{:S(2)}) collective-permute-start(f32[4,8,1536]{2,1,0:T(8,128)} %pad_maximum_fusion.7), channel_id=1, source_target_pairs={{0,1},{1,2},{2,3},{3,4},{4,5},{5,6},{6,7},{7,8},{8,9},{9,10},{10,1... | collective-permute-start | bytes 589832 | tf_op jit(solution)/shard_map/ppermute | solution.py:19
  49.1 8.8 %collective-permute-start.3 = (f32[1,8,1536]{2,1,0:T(8,128)S(1)}, f32[1,8,1536]{2,1,0:T(8,128)}, u32[]{:S(2)}, u32[]{:S(2)}) collective-permute-start(f32[1,8,1536]{2,1,0:T(8,128)S(1)} %get-tuple-element.40), channel_id=1, source_target_pairs={{0,8},{1,9},{2,10},{3,11},{4,12},{5,13},{6,14},{7,15},{8,16},{9,17... | collective-permute-start | bytes 147464 | tf_op jit(solution)/shard_map/ppermute | solution.py:19
  57.9 6.3 %collective-permute-start.7 = (f32[1,8,1536]{2,1,0:T(8,128)S(1)}, f32[1,8,1536]{2,1,0:T(8,128)S(1)}, u32[]{:S(2)}, u32[]{:S(2)}) collective-permute-start(f32[1,8,1536]{2,1,0:T(8,128)S(1)} %get-tuple-element.32), channel_id=1, source_target_pairs={{8,0},{9,1},{10,2},{11,3},{12,4},{13,5},{14,6},{15,7},{16,8},{17,9... | collective-permute-start | bytes 147464 | tf_op jit(solution)/shard_map/ppermute | solution.py:19
  64.5 1.1 copy.37
  65.6 1.3 divide_reduce_fusion
  66.9 1.2 constant_dynamic-update-slice_fusion
  68.1 7.3 %pmin.28 = f32[]{:T(128)} all-reduce(f32[]{:T(128)} %divide_reduce_fusion), channel_id=1, replica_groups=mesh['patch_0'=4,'patch_1'=4,'patch_2'=16,'patch_3'=2] {'patch_0'}, use_global_device_ids=true, to_apply=%region_2.0 | all-reduce | flops 1 | bytes 8 | tf_op jit(solution)/shard_map/pmin | solution.py:24
  75.5 7.3 %pmin.29 = f32[]{:T(128)} all-reduce(f32[]{:T(128)} %pmin.28), channel_id=1, replica_groups=mesh['patch_0'=4,'patch_1'=4,'patch_2'=16,'patch_3'=2] {'patch_1'}, use_global_device_ids=true, to_apply=%region_3.0 | all-reduce | flops 1 | bytes 8 | tf_op jit(solution)/shard_map/pmin | solution.py:24
  83.0 26.9 %pmin.30 = f32[]{:T(128)} all-reduce(f32[]{:T(128)} %pmin.29), channel_id=1, replica_groups=mesh['patch_0'=4,'patch_1'=4,'patch_2'=16,'patch_3'=2] {'patch_2'}, use_global_device_ids=true, to_apply=%region_4.0 | all-reduce | flops 1 | bytes 8 | tf_op jit(solution)/shard_map/pmin | solution.py:24
  110.1 13.9 %pmin.31 = f32[]{:T(128)} all-reduce(f32[]{:T(128)} %pmin.30), channel_id=1, replica_groups=mesh['patch_0'=4,'patch_1'=4,'patch_2'=16,'patch_3'=2] {'patch_3'}, use_global_device_ids=true, to_apply=%region_5.0 | all-reduce | flops 1 | bytes 8 | tf_op jit(solution)/shard_map/pmin | solution.py:24
  124.6 0.7 broadcast_divide_fusion
  125.3 0.9 fusion.30
  126.2 1.9 collective-permute-start.5
  128.2 3.4 %collective-permute-start.1 = (f32[4,8,1536]{2,1,0:T(8,128)S(1)}, f32[4,8,1536]{2,1,0:T(8,128)S(1)}, u32[]{:S(2)}, u32[]{:S(2)}) collective-permute-start(f32[4,8,1536]{2,1,0:T(8,128)S(1)} %pad_maximum_fusion.8), channel_id=1, source_target_pairs={{0,2},{1,3},{2,4},{3,5},{4,6},{5,7},{6,8},{7,9},{8,10},{9,11},{10,... | collective-permute-start | bytes 589832 | tf_op jit(solution)/shard_map/ppermute | solution.py:19
  131.6 2.6 %collective-permute-done.5 = f32[4,8,1536]{2,1,0:T(8,128)S(1)} collective-permute-done((f32[4,8,1536]{2,1,0:T(8,128)S(1)}, f32[4,8,1536]{2,1,0:T(8,128)S(1)}, u32[]{:S(2)}, u32[]{:S(2)}) %collective-permute-start.5) | collective-permute-done | bytes 196640 | tf_op jit(solution)/shard_map/ppermute | solution.py:19
  134.3 11.0 %collective-permute-start.6 = (f32[4,8,1536]{2,1,0:T(8,128)S(1)}, f32[4,8,1536]{2,1,0:T(8,128)S(1)}, u32[]{:S(2)}, u32[]{:S(2)}) collective-permute-start(f32[4,8,1536]{2,1,0:T(8,128)S(1)} %pad_maximum_fusion.12), channel_id=1, source_target_pairs={{4,0},{5,1},{6,2},{7,3},{8,4},{9,5},{10,6},{11,7},{12,8},{13,9},{1... | collective-permute-start | bytes 589832 | tf_op jit(solution)/shard_map/ppermute | solution.py:19
  145.3 2.1 %collective-permute-start.2 = (f32[4,8,1536]{2,1,0:T(8,128)S(1)}, f32[4,8,1536]{2,1,0:T(8,128)S(1)}, u32[]{:S(2)}, u32[]{:S(2)}) collective-permute-start(f32[4,8,1536]{2,1,0:T(8,128)S(1)} %pad_maximum_fusion.9), channel_id=1, source_target_pairs={{0,4},{1,5},{2,6},{3,7},{4,8},{5,9},{6,10},{7,11},{8,12},{9,13},{1... | collective-permute-start | bytes 589832 | tf_op jit(solution)/shard_map/ppermute | solution.py:19
  147.5 15.7 %collective-permute-done.2 = f32[4,8,1536]{2,1,0:T(8,128)S(1)} collective-permute-done((f32[4,8,1536]{2,1,0:T(8,128)S(1)}, f32[4,8,1536]{2,1,0:T(8,128)S(1)}, u32[]{:S(2)}, u32[]{:S(2)}) %collective-permute-start.2) | collective-permute-done | bytes 196640 | tf_op jit(solution)/shard_map/ppermute | solution.py:19
  163.3 0.8 copy_dynamic-update-slice_fusion.8
  164.4 10.4 %gather_fusion.1 = f32[1024,384]{1,0:T(8,128)} fusion(f32[256,4,384]{2,1,0:T(4,128)S(1)} %copy_dynamic-update-slice_fusion, s32[1024]{0:T(1024)S(1)} %reshape.152), kind=kCustom, calls=%fused_computation.1 | custom fusion | bytes 3153920 | tf_op jit(solution)/shard_map/gather | solution.py:143
  174.8 2.5 %reshape.139 = f32[128,4,2,4,96]{4,3,2,1,0:T(4,128)S(1)} reshape(f32[1024,384]{1,0:T(8,128)} %gather_fusion.1) | data formatting | bytes 3145728 | tf_op jit(solution)/shard_map/reshape | solution.py:144
  177.3 2.5 %slice.493 = f32[128,4,2,4,32]{4,3,2,1,0:T(4,128)} slice(f32[128,4,2,4,96]{4,3,2,1,0:T(4,128)S(1)} %reshape.139), slice={[0:128], [0:4], [0:2], [0:4], [64:96]} | slice | bytes 1048576 | tf_op jit(solution)/shard_map/slice | solution.py:146
  179.8 1.7 copy.55
  181.5 1.2 copy.72
  182.7 1.0 slice_bitcast_fusion.3
  183.7 2.0 copy.73
  186.3 0.7 copy-done.5
  187.7 0.9 fusion.13
  189.7 0.8 fusion.3
  190.6 1.7 slice_subtract_fusion.3
  192.8 0.9 fusion.15
  194.8 0.7 fusion.1
  195.5 0.9 copy-done.6
  196.3 3.0 %fusion.11 = f32[4,32,32,128]{3,2,1,0:T(8,128)} fusion(f32[4,32,32,128]{3,2,1,0:T(8,128)S(1)} %copy-done.1, f32[4,33,32,128]{3,1,2,0:T(8,128)S(1)} %fusion.1, f32[4,32,32,128]{3,1,2,0:T(8,128)S(1)} %copy-done.6, f32[128]{0:T(128)S(1)} %broadcast_divide_fusion), kind=kLoop, calls=%fused_computation.24 | loop fusion | flops 2097152 | bytes 10486272 | tf_op jit(solution)/shard_map/sub | solution.py:108
  (93 shorter events, 5.8 us)
Async XLA Ops:
  0.6 3.0 %copy-start = (f32[4,32,32,128]{3,2,1,0:T(8,128)S(1)}, f32[4,32,32,128]{3,2,1,0:T(8,128)}, u32[]{:S(2)}) copy-start(f32[4,32,32,128]{3,2,1,0:T(8,128)} %param.8) | copy-start | bytes 6291460
  3.6 1.3 copy-start.2
  5.1 31.8 %copy-start.4 = (f32[128,4,4,4,32]{0,4,3,2,1:T(8,128)}, f32[128,4,4,4,32]{0,4,3,2,1:T(8,128)S(1)}, u32[]{:S(2)}) copy-start(f32[128,4,4,4,32]{0,4,3,2,1:T(8,128)S(1)} %maximum_bitcast_fusion) | copy-start | bytes 3145732
  34.7 3.6 %copy-start.8 = (s32[1,16,8]{1,2,0:T(8,128)S(1)}, s32[1,16,8]{1,2,0:T(8,128)}, u32[]{:S(2)}) copy-start(s32[1,16,8]{1,2,0:T(8,128)} %param.13) | copy-start | bytes 1540
  40.3 24.2 %copy-start.7 = (f32[128,4,4,96]{0,3,2,1:T(8,128)S(1)}, f32[128,4,4,96]{0,3,2,1:T(8,128)}, u32[]{:S(2)}) copy-start(f32[128,4,4,96]{0,3,2,1:T(8,128)} %pad_maximum_fusion.4) | copy-start | bytes 2359300
  40.3 25.3 %copy-start.10 = (s32[128,4]{0,1:T(4,128)S(1)}, s32[128,4]{0,1:T(4,128)}, u32[]{:S(2)}) copy-start(s32[128,4]{0,1:T(4,128)} %param.11) | copy-start | bytes 6148
  40.3 25.4 %copy-start.11 = (s32[128,4]{0,1:T(4,128)S(1)}, s32[128,4]{0,1:T(4,128)}, u32[]{:S(2)}) copy-start(s32[128,4]{0,1:T(4,128)} %param.10) | copy-start | bytes 6148
  42.2 40.5 %copy-start.9 = (s32[128,4,2]{0,2,1:T(2,128)S(1)}, s32[128,4,2]{0,2,1:T(2,128)}, u32[]{:S(2)}) copy-start(s32[128,4,2]{0,2,1:T(2,128)} %param.12) | copy-start | bytes 12292
  42.2 40.5 %copy-start.13 = (s32[4]{0:T(128)S(1)}, s32[4]{0:T(128)}, u32[]{:S(2)}) copy-start(s32[4]{0:T(128)} %constant.81) | copy-start | bytes 52
  42.2 83.1 %collective-permute-start.4 = (f32[4,8,1536]{2,1,0:T(8,128)}, f32[4,8,1536]{2,1,0:T(8,128)}, u32[]{:S(2)}, u32[]{:S(2)}) collective-permute-start(f32[4,8,1536]{2,1,0:T(8,128)} %pad_maximum_fusion.10), channel_id=1, source_target_pairs={{1,0},{2,1},{3,2},{4,3},{5,4},{6,5},{7,6},{8,7},{9,8},{10,9},{11,1... | collective-permute-start | bytes 589832 | tf_op jit(solution)/shard_map/ppermute | solution.py:19
  45.6 82.5 %collective-permute-start = (f32[4,8,1536]{2,1,0:T(8,128)}, f32[4,8,1536]{2,1,0:T(8,128)S(1)}, u32[]{:S(2)}, u32[]{:S(2)}) collective-permute-start(f32[4,8,1536]{2,1,0:T(8,128)} %pad_maximum_fusion.7), channel_id=1, source_target_pairs={{0,1},{1,2},{2,3},{3,4},{4,5},{5,6},{6,7},{7,8},{8,9},{9,10},{10,1... | collective-permute-start | bytes 589832 | tf_op jit(solution)/shard_map/ppermute | solution.py:19
  49.1 114.2 %collective-permute-start.3 = (f32[1,8,1536]{2,1,0:T(8,128)S(1)}, f32[1,8,1536]{2,1,0:T(8,128)}, u32[]{:S(2)}, u32[]{:S(2)}) collective-permute-start(f32[1,8,1536]{2,1,0:T(8,128)S(1)} %get-tuple-element.40), channel_id=1, source_target_pairs={{0,8},{1,9},{2,10},{3,11},{4,12},{5,13},{6,14},{7,15},{8,16},{9,17... | collective-permute-start | bytes 147464 | tf_op jit(solution)/shard_map/ppermute | solution.py:19
  57.9 106.5 %collective-permute-start.7 = (f32[1,8,1536]{2,1,0:T(8,128)S(1)}, f32[1,8,1536]{2,1,0:T(8,128)S(1)}, u32[]{:S(2)}, u32[]{:S(2)}) collective-permute-start(f32[1,8,1536]{2,1,0:T(8,128)S(1)} %get-tuple-element.32), channel_id=1, source_target_pairs={{8,0},{9,1},{10,2},{11,3},{12,4},{13,5},{14,6},{15,7},{16,8},{17,9... | collective-permute-start | bytes 147464 | tf_op jit(solution)/shard_map/ppermute | solution.py:19
  126.2 8.0 %collective-permute-start.5 = (f32[4,8,1536]{2,1,0:T(8,128)S(1)}, f32[4,8,1536]{2,1,0:T(8,128)S(1)}, u32[]{:S(2)}, u32[]{:S(2)}) collective-permute-start(f32[4,8,1536]{2,1,0:T(8,128)S(1)} %pad_maximum_fusion.11), channel_id=1, source_target_pairs={{2,0},{3,1},{4,2},{5,3},{6,4},{7,5},{8,6},{9,7},{10,8},{11,9},{12,... | collective-permute-start | bytes 589832 | tf_op jit(solution)/shard_map/ppermute | solution.py:19
  128.2 17.1 %collective-permute-start.1 = (f32[4,8,1536]{2,1,0:T(8,128)S(1)}, f32[4,8,1536]{2,1,0:T(8,128)S(1)}, u32[]{:S(2)}, u32[]{:S(2)}) collective-permute-start(f32[4,8,1536]{2,1,0:T(8,128)S(1)} %pad_maximum_fusion.8), channel_id=1, source_target_pairs={{0,2},{1,3},{2,4},{3,5},{4,6},{5,7},{6,8},{7,9},{8,10},{9,11},{10,... | collective-permute-start | bytes 589832 | tf_op jit(solution)/shard_map/ppermute | solution.py:19
  134.3 29.9 %collective-permute-start.6 = (f32[4,8,1536]{2,1,0:T(8,128)S(1)}, f32[4,8,1536]{2,1,0:T(8,128)S(1)}, u32[]{:S(2)}, u32[]{:S(2)}) collective-permute-start(f32[4,8,1536]{2,1,0:T(8,128)S(1)} %pad_maximum_fusion.12), channel_id=1, source_target_pairs={{4,0},{5,1},{6,2},{7,3},{8,4},{9,5},{10,6},{11,7},{12,8},{13,9},{1... | collective-permute-start | bytes 589832 | tf_op jit(solution)/shard_map/ppermute | solution.py:19
  145.3 17.9 %collective-permute-start.2 = (f32[4,8,1536]{2,1,0:T(8,128)S(1)}, f32[4,8,1536]{2,1,0:T(8,128)S(1)}, u32[]{:S(2)}, u32[]{:S(2)}) collective-permute-start(f32[4,8,1536]{2,1,0:T(8,128)S(1)} %pad_maximum_fusion.9), channel_id=1, source_target_pairs={{0,4},{1,5},{2,6},{3,7},{4,8},{5,9},{6,10},{7,11},{8,12},{9,13},{1... | collective-permute-start | bytes 589832 | tf_op jit(solution)/shard_map/ppermute | solution.py:19
  185.7 1.2 copy-start.5
  185.7 1.2 copy-start.12
  186.0 1.7 copy-start.3
  190.6 2.2 %copy-start.1 = (f32[4,32,32,128]{3,2,1,0:T(8,128)S(1)}, f32[4,32,32,128]{3,2,1,0:T(8,128)}, u32[]{:S(2)}) copy-start(f32[4,32,32,128]{3,2,1,0:T(8,128)} %param.8) | copy-start | bytes 6291460
  194.8 1.6 copy-start.6
where the time goes:
time: 201 us; the launch traced here: 200 us
  local copies, waits for them, and re-layouts  67.6 us (34%)
  blocking collectives  55.3 us (28%)
  starting transfers between devices  39.6 us (20%)
  waiting for transfers between devices  18.3 us (9%)
  other arithmetic  16.6 us (8%)
  between operations  3.03 us (2%)
    pmin x4, blocking collectives, one_axis_at_a_time(): array = lax.pmin(array, axis)  55.3 us
    ppermute x8, starting transfers between devices, from_behind(): return lax.ppermute(array, axis, pairs)  39.6 us
    ppermute x8, waiting for transfers between devices, from_behind(): return lax.ppermute(array, axis, pairs)  18.3 us
    gather x1, local copies, waits for them, and re-layouts, on_device(): picked = ghost_pool.reshape(ghost_pool.shape[0], 4, -1)[neighbour, opposite]  10.4 us
    slice x2, local copies, waits for them, and re-layouts, restrict(): total = strip[..., 0::2, 0::2] + strip[..., 1::2, 0::2]  10.4 us
    slice x1, local copies, waits for them, and re-layouts, restrict(): total = total + strip[..., 1::2, 1::2]  9.65 us
    slice x1, local copies, waits for them, and re-layouts, restrict(): total = total + strip[..., 0::2, 1::2]  9.56 us
    unnamed x45, local copies, waits for them, and re-layouts  8.78 us
  transfers between devices with their start and end apart: 8, of which 2 were waited for; matrix products, arithmetic and copies ran while one was open for 4% of the time, Pallas kernels for 0%

commit v1 on v0

v1 whole, which is shorter than its diff:
```python
import jax
import jax.numpy as jnp
from jax import lax
from jax.experimental import pallas as pl
from jax.experimental.pallas import tpu as pltpu
from jax.sharding import Mesh
from jax.sharding import PartitionSpec as P

AXES = ("patch_0", "patch_1", "patch_2", "patch_3")
SHAPE = (4, 4, 16, 2)
COURANT = 0.4
CHUNKS = 8
NEAR = 64
ROWS = 80
PACK = 16 * ROWS
TILES = PACK // 128
LINE = 36
SPAN = 1160
F32 = jnp.float32
VMEM = pl.BlockSpec(memory_space=pltpu.VMEM)
ANY = pl.BlockSpec(memory_space=pl.ANY)


def spacing_of(level):
    return jnp.where(level == 6, 1.0, jnp.where(level == 5, 2.0, 4.0)).astype(F32)


def start_fields(fields, cells, sems, lead):
    width = 1024 // CHUNKS
    copies = []
    for chunk in range(CHUNKS):
        copy = pltpu.make_async_copy(
            fields.at[:, pl.ds(chunk * width, width)],
            cells.at[:, pl.ds(32 * lead + chunk * width, width)],
            sems.at[chunk],
        )
        copy.start()
        copies.append(copy)
    return copies


def core_index():
    return lax.axis_index("patch_3")


def pack_kernel(fields, level, send, own, swap, least, rows, cells, sems):
    copies = start_fields(fields, cells, sems, 0)
    width = 32 // CHUNKS
    fastest = jnp.zeros((32, 128), F32)
    for chunk in range(CHUNKS):
        copies[chunk].wait()

        def speeds(x, best):
            h, m, n = [cells[c, pl.ds(pl.multiple_of(32 * x, 32), 32), :] for c in range(3)]
            v = jnp.maximum(jnp.abs(m), jnp.abs(n)) / h
            return jnp.maximum(best, v + jnp.sqrt(h))

        fastest = lax.fori_loop(chunk * width, (chunk + 1) * width, speeds, fastest, unroll=True)
    top = jnp.max(fastest, axis=0, keepdims=True)
    ratio = spacing_of(level[...]) / top
    least[...] = jnp.broadcast_to(jnp.min(ratio, axis=1, keepdims=True), least.shape)

    for face in range(4):
        for c in range(4):
            base = (face * 4 + c) * ROWS
            at = [k if face % 2 == 0 else 31 - k for k in range(4)]
            for k in range(2):
                if face < 2:
                    line = cells[c, pl.ds(32 * at[k], 32), :]
                else:
                    line = cells[c, pl.ds(at[k], 32, stride=32), :]
                rows[pl.ds(base + 32 * k, 32), :] = line
            if face < 2:
                take = lambda k, odd: cells[c, pl.ds(at[k] * 32 + odd, 16, stride=2), :]
            else:
                take = lambda k, odd: cells[c, pl.ds(odd * 32 + at[k], 16, stride=64), :]
            total = take(2, 0) + take(3, 0)
            total = total + take(2, 1)
            total = total + take(3, 1)
            rows[pl.ds(base + NEAR, 16), :] = 0.25 * total

    lane = lax.broadcasted_iota(jnp.int32, (16, 128), 1)
    block = lax.broadcasted_iota(jnp.int32, (16, 128), 0)
    spread = jnp.where(((lane // 8) ^ (8 * core_index())) == block, 1.0, 0.0).astype(F32)
    listed = jnp.dot(send[...].astype(F32), spread, preferred_element_type=F32)
    slot = lax.broadcasted_iota(jnp.int32, (8, 128), 0)
    mine = (lax.broadcasted_iota(jnp.int32, (8, 128), 1) % 8) == slot
    chosen = jnp.sum(jnp.where(mine, listed, 0.0), axis=0, keepdims=True).astype(jnp.int32)
    index = jnp.broadcast_to(chosen, (128, 128))
    for tile in range(TILES):
        picked = jnp.take_along_axis(rows[pl.ds(tile * 128, 128), :], index, axis=1)
        turned = picked.T
        swap[80 + tile] = turned[0:8]
        for j in range(1, 8):
            own[(j - 1) * TILES + tile] = turned[8 * j : 8 * j + 8]
        for j in range(8):
            swap[j * TILES + tile] = turned[64 + 8 * j : 72 + 8 * j]


def pack(fields, level, send):
    return pl.pallas_call(
        pack_kernel,
        out_shape=(
            jax.ShapeDtypeStruct((70, 8, 128), F32),
            jax.ShapeDtypeStruct((90, 8, 128), F32),
            jax.ShapeDtypeStruct((lax.axis_size("patch_2"), 128), F32),
            jax.ShapeDtypeStruct((PACK, 128), F32),
        ),
        in_specs=[ANY, VMEM, VMEM],
        out_specs=(VMEM, VMEM, VMEM, VMEM),
        scratch_shapes=[pltpu.VMEM((4, 1024, 128), F32), pltpu.SemaphoreType.DMA((CHUNKS,))],
        name="pack",
    )(fields, level, send)


def least_kernel(got, out):
    low = jnp.min(jnp.min(got[...], axis=0, keepdims=True), axis=1, keepdims=True)
    out[...] = jnp.broadcast_to(low, out.shape)


def spread_least(got, members):
    return pl.pallas_call(
        least_kernel,
        out_shape=jax.ShapeDtypeStruct((members, 128), F32),
        in_specs=[VMEM],
        out_specs=VMEM,
        name="least",
    )(got)


def physical(q, normal):
    h = q[0]
    m = q[normal]
    v = m / h
    flux = [m, q[1] * v, q[2] * v, q[3] * v]
    flux[normal] = flux[normal] + 0.5 * h * h
    return flux, jnp.abs(v) + jnp.sqrt(h)


def interface(left, right, normal):
    lf, ls = physical(left, normal)
    rf, rs = physical(right, normal)
    widest = 0.5 * jnp.maximum(ls, rs)
    return [0.5 * (lf[c] + rf[c]) - widest * (right[c] - left[c]) for c in range(4)]


def step_kernel(
    fields, rows, r1, r2, r3, r4, w, q, got, level, relation, half, refs,
    out, step, cells, lines, fluxes, pool, edge, weave, sems,
):
    copies = start_fields(fields, cells, sems, 2)
    b8 = TILES
    sources = [
        (r1, b8), (r1, 0), (r2, b8), (r2, 0), (r3, b8), (r3, 0), (r4, b8), (r4, 0),
        (w, 80), (q, b8), (q, 0), (q, 3 * b8), (q, 2 * b8), (q, 5 * b8), (q, 4 * b8), (q, 6 * b8),
    ]
    for tile in range(TILES):
        joined = jnp.concatenate([ref[at + tile] for ref, at in sources], axis=0)
        pool[pl.ds(tile * 128, 128), :] = joined.T

    for copy in copies:
        copy.wait()

    def lay(x, carry):
        for c in range(4):
            line = cells[c, pl.ds(pl.multiple_of(32 * x + 64, 32), 32), :]
            lines[pl.ds(c * SPAN + x * LINE + 2, 32), :] = line
        return carry

    lax.fori_loop(0, 32, lay, 0, unroll=4)

    flip = 64 * core_index()
    for face in range(4):
        kind = relation[pl.ds(face, 1), :]
        upper = half[pl.ds(face, 1), :] == 1
        names = [refs[pl.ds(2 * face + m, 1), :] for m in range(2)]
        away = [name >= 128 for name in names]
        local = [name & 127 for name in names]
        remote = [(name & 127) ^ flip for name in names]

        def gather(own_rows, pool_rows, m):
            shape = own_rows.shape
            a = jnp.take_along_axis(own_rows, jnp.broadcast_to(local[m], shape), axis=1)
            b = jnp.take_along_axis(pool_rows, jnp.broadcast_to(remote[m], shape), axis=1)
            return jnp.where(away[m], b, a)

        for c in range(4):
            base = ((face ^ 1) * 4 + c) * ROWS

            def coarse_first(ref):
                total = ref[pl.ds(base, 16, stride=2), :] + ref[pl.ds(base + 32, 16, stride=2), :]
                total = total + ref[pl.ds(base + 1, 16, stride=2), :]
                total = total + ref[pl.ds(base + 33, 16, stride=2), :]
                return 0.25 * total

            near = gather(rows[pl.ds(base, NEAR), :], pool[pl.ds(base, NEAR), :], 0)
            fine = [[], []]
            pairs = [
                (coarse_first(rows), coarse_first(pool)),
                (rows[pl.ds(base + NEAR, 16), :], pool[pl.ds(base + NEAR, 16), :]),
            ]
            for g in range(2):
                fine[g] = jnp.concatenate([gather(*pairs[g], 0), gather(*pairs[g], 1)], axis=0)
            column = near[0:32]
            edge[pl.ds(1, 32), :] = column
            edge[pl.ds(0, 1), :] = column[0:1]
            edge[pl.ds(33, 1), :] = column[31:32]
            slope = edge[pl.ds(2, 32), :] - edge[pl.ds(0, 32), :]
            value = jnp.where(upper, column[16:32], column[0:16])
            tilt = 0.125 * jnp.where(upper, slope[16:32], slope[0:16])
            weave[pl.ds(0, 16, stride=2), :] = value - tilt
            weave[pl.ds(1, 16, stride=2), :] = value + tilt
            coarse = weave[...]
            sign = -1.0 if c == 1 + face // 2 else 1.0
            for g in range(2):
                mirror = sign * rows[pl.ds((face * 4 + c) * ROWS + 32 * g, 32), :]
                ghost = jnp.where(
                    kind == 0,
                    mirror,
                    jnp.where(
                        kind == 1,
                        near[32 * g : 32 * g + 32],
                        jnp.where(kind == 2, coarse, fine[g]),
                    ),
                )
                at = 1 - g if face % 2 == 0 else 34 + g
                if face < 2:
                    cells[c, pl.ds(32 * at, 32), :] = ghost
                else:
                    lines[pl.ds(c * SPAN + at, 32, stride=LINE), :] = ghost

    def along_y(n, carry):
        r = 1 + 8 * n
        left, right = [], []
        for c in range(4):
            before, here, after, beyond = [
                lines[pl.ds(c * SPAN + r + d, 8), :] for d in (-1, 0, 1, 2)
            ]
            left.append(here + 0.25 * (after - before))
            right.append(after - 0.25 * (beyond - here))
        flux = interface(left, right, 2)
        for c in range(4):
            fluxes[pl.ds(c * SPAN + r, 8), :] = flux[c]
        return carry

    lax.fori_loop(0, 144, along_y, 0, unroll=4)

    low = jnp.min(jnp.min(got[...], axis=0, keepdims=True), axis=1, keepdims=True)
    chosen = COURANT * low
    step[...] = chosen
    ratio = chosen / spacing_of(level[...])

    for part in range(4):
        y = 8 * part

        def load(x):
            return [cells[c, pl.ds(pl.multiple_of(32 * x + y, 8), 8), :] for c in range(4)]

        def along_x(i, carry):
            here, ahead, left, last = carry
            beyond = load(i + 3)
            lean = [0.25 * (beyond[c] - here[c]) for c in range(4)]
            right = [ahead[c] - lean[c] for c in range(4)]
            flux = interface(left, right, 1)
            if last is not None:
                for c in range(4):
                    at = c * SPAN + (i - 1) * LINE + y
                    change = (flux[c] - last[c]) + (
                        fluxes[pl.ds(at + 2, 8), :] - fluxes[pl.ds(at + 1, 8), :]
                    )
                    to = pl.multiple_of(32 * (i - 1) + y, 8)
                    out[c, pl.ds(to, 8), :] = here[c] - ratio * change
            return ahead, beyond, [ahead[c] + lean[c] for c in range(4)], flux

        first, second, third = load(0), load(1), load(2)
        left = [second[c] + 0.25 * (third[c] - first[c]) for c in range(4)]
        state = along_x(0, (second, third, left, None))
        lax.fori_loop(1, 33, along_x, state, unroll=4)


def advance(*operands):
    return pl.pallas_call(
        step_kernel,
        out_shape=(
            jax.ShapeDtypeStruct((4, 1024, 128), F32),
            jax.ShapeDtypeStruct((1, 1), F32),
        ),
        in_specs=[ANY] + [VMEM] * 12,
        out_specs=(VMEM, VMEM),
        scratch_shapes=[
            pltpu.VMEM((4, 36 * 32, 128), F32),
            pltpu.VMEM((4 * SPAN, 128), F32),
            pltpu.VMEM((4 * SPAN, 128), F32),
            pltpu.VMEM((PACK, 128), F32),
            pltpu.VMEM((40, 128), F32),
            pltpu.VMEM((32, 128), F32),
            pltpu.SemaphoreType.DMA((CHUNKS,)),
        ],
        name="advance",
    )(*operands)


def two_way(array, chips):
    n = lax.axis_size(AXES)
    pairs = [(i, (i + (2 * chips if i % 2 == 0 else -2 * chips)) % n) for i in range(n)]
    return lax.ppermute(array, AXES, pairs)


def swap_cores(array):
    return lax.ppermute(array, AXES, [(i, i ^ 1) for i in range(lax.axis_size(AXES))])


def on_device(fields, patch_level, relation, face_half, neighbour, send_list):
    level = patch_level.reshape(1, 128)
    flat = fields.reshape(4, 1024, 128)
    own, swap, least, rows = pack(flat, level, send_list[0].T)
    w = swap_cores(swap)

    def blk(array, n):
        return array[n * TILES : (n + 1) * TILES]

    moved = []
    for chips in range(1, 5):
        a = 2 * chips - 2
        parts = [blk(own, a), blk(w, a)]
        if chips < 4:
            parts.append(blk(own, a + 1))
        parts.append(blk(w, a + 1))
        moved.append(two_way(jnp.concatenate(parts), chips))
    q = swap_cores(jnp.concatenate([array[2 * TILES :] for array in moved]))
    got = lax.all_to_all(least, ("patch_2",), 0, 0, tiled=True)
    others = ("patch_0", "patch_1", "patch_3")
    got = lax.all_to_all(spread_least(got, lax.axis_size(others)), others, 0, 0, tiled=True)
    advanced, step = advance(
        flat, rows, *moved, w, q, got, level, relation.T, face_half.T,
        neighbour.transpose(1, 2, 0).reshape(8, 128),
    )
    return advanced.reshape(fields.shape), step[0, 0]


def solution(mesh):
    split = Mesh(mesh.devices.reshape(SHAPE), AXES)
    return jax.shard_map(
        on_device,
        mesh=split,
        in_specs=(
            P(None, None, None, AXES),
            P(AXES),
            P(AXES, None),
            P(AXES, None),
            P(AXES, None, None),
            P(AXES, None, None),
        ),
        out_specs=(P(None, None, None, AXES), P()),
        check_vma=False,
    )
```

time: 201 us -> 91.7 us (0.46)
  the two profiles are of different devices: /device:TPU:41 before, /device:TPU:1 now
where the time goes in v1:
time: 91.7 us; the launch traced here: 91.1 us
  starting transfers between devices  31.7 us (35%)
  blocking collectives  31.5 us (34%)
  Pallas kernels  14.7 us (16%)
  waiting for transfers between devices  10.5 us (11%)
  local copies, waits for them, and re-layouts  1.68 us (2%)
    ppermute x4, starting transfers between devices, two_way(): return lax.ppermute(array, AXES, pairs)  21 us
    all_to_all x1, blocking collectives, on_device(): lax.all_to_all(spread_least(got, lax.axis_size(others)), others, 0, 0, ti...  16.2 us
    all_to_all x1, blocking collectives, on_device(): got = lax.all_to_all(least, ('patch_2',), 0, 0, tiled=True)  15.3 us
    ppermute x2, starting transfers between devices, swap_cores(): lax.ppermute(array, AXES, [(i, i ^ 1) for i in range(lax.axis_size(AXES))])  10.7 us
    ppermute x4, waiting for transfers between devices, two_way(): return lax.ppermute(array, AXES, pairs)  9.93 us
    pallas_call x1, Pallas kernels, advance(): pl.pallas_call(step_kernel, out_shape=(jax.ShapeDtypeStruct((4, 1024, 128...  9.55 us
    pallas_call x1, Pallas kernels, pack(): pl.pallas_call(pack_kernel, out_shape=(jax.ShapeDtypeStruct((70, 8, 128),...  3.81 us
  transfers between devices with their start and end apart: 6, of which 2 were waited for; matrix products, arithmetic and copies ran while one was open for 1% of the time, Pallas kernels for 2%

profile of v1, /device:TPU:1, one launch (start us, length us, event | category | flops | bytes accessed | tf_op | source)
XLA Modules:
  0.0 91.1 jit_solution(4249959115470892519)
XLA Ops:
  0.6 3.8 %pack.1 = (f32[70,8,128]{2,1,0:T(8,128)}, f32[90,8,128]{2,1,0:T(8,128)}, f32[16,128]{1,0:T(8,128)}, f32[1280,128]{1,0:T(8,128)}) custom-call(f32[4,1024,128]{2,1,0:T(8,128)} %bitcast.20, s32[1,128]{1,0:T(1,128)} %bitcast.30, s32[8,16]{1,0:T(8,128)} %bitcast.26), custom_call_target="tpu_custom_call" | custom-call | tf_op jit(solution)/shard_map/pack/pallas_call | solution.py:101
  4.4 0.0 copy-start.6
  4.5 8.7 %collective-permute-start = (f32[90,8,128]{2,1,0:T(8,128)}, f32[90,8,128]{2,1,0:T(8,128)S(1)}, u32[]{:S(2)}, u32[]{:S(2)}) collective-permute-start(f32[90,8,128]{2,1,0:T(8,128)} %get-tuple-element.10), channel_id=1, source_target_pairs={{0,1},{1,0},{2,3},{3,2},{4,5},{5,4},{6,7},{7,6},{8,9},{9,8},{10,11... | collective-permute-start | bytes 1105928 | tf_op jit(solution)/shard_map/ppermute | solution.py:310
  13.2 0.9 %fusion.1 = (f32[10,8,128]{2,1,0:T(8,128)S(1)}, f32[10,8,128]{2,1,0:T(8,128)S(1)}, f32[10,8,128]{2,1,0:T(8,128)S(1)}, f32[10,8,128]{2,1,0:T(8,128)S(1)}, f32[10,...) fusion(f32[70,8,128]{2,1,0:T(8,128)} %get-tuple-element.9), kind=kLoop, calls=%fused_computation.6 | loop fusion | bytes 573440 | tf_op jit(solution)/shard_map/slice | solution.py:320
  14.1 0.6 collective-permute-done.w
  14.7 0.0 copy-start
  14.8 10.4 %collective-permute-start.1 = (f32[40,8,128]{2,1,0:T(8,128)S(1)}, f32[40,8,128]{2,1,0:T(8,128)S(1)}, u32[]{:S(2)}, u32[]{:S(2)}) collective-permute-start(f32[40,8,128]{2,1,0:T(8,128)S(1)} %pad_maximum_fusion.1), channel_id=1, source_target_pairs={{0,2},{1,511},{2,4},{3,1},{4,6},{5,3},{6,8},{7,5},{8,10},{9,7},{10... | collective-permute-start | bytes 491528 | tf_op jit(solution)/shard_map/ppermute | solution.py:306
  25.2 3.1 %collective-permute-start.2 = (f32[40,8,128]{2,1,0:T(8,128)S(1)}, f32[40,8,128]{2,1,0:T(8,128)S(1)}, u32[]{:S(2)}, u32[]{:S(2)}) collective-permute-start(f32[40,8,128]{2,1,0:T(8,128)S(1)} %pad_maximum_fusion.2), channel_id=1, source_target_pairs={{0,4},{1,509},{2,6},{3,511},{4,8},{5,1},{6,10},{7,3},{8,12},{9,5},... | collective-permute-start | bytes 491528 | tf_op jit(solution)/shard_map/ppermute | solution.py:306
  28.3 4.7 %collective-permute-start.3 = (f32[40,8,128]{2,1,0:T(8,128)S(1)}, f32[40,8,128]{2,1,0:T(8,128)S(1)}, u32[]{:S(2)}, u32[]{:S(2)}) collective-permute-start(f32[40,8,128]{2,1,0:T(8,128)S(1)} %pad_maximum_fusion.3), channel_id=1, source_target_pairs={{0,6},{1,507},{2,8},{3,509},{4,10},{5,511},{6,12},{7,1},{8,14},{9,... | collective-permute-start | bytes 491528 | tf_op jit(solution)/shard_map/ppermute | solution.py:306
  33.1 2.8 %collective-permute-start.4 = (f32[30,8,128]{2,1,0:T(8,128)S(1)}, f32[30,8,128]{2,1,0:T(8,128)S(1)}, u32[]{:S(2)}, u32[]{:S(2)}) collective-permute-start(f32[30,8,128]{2,1,0:T(8,128)S(1)} %pad_maximum_fusion.4), channel_id=1, source_target_pairs={{0,8},{1,505},{2,10},{3,507},{4,12},{5,509},{6,14},{7,511},{8,16},... | collective-permute-start | bytes 368648 | tf_op jit(solution)/shard_map/ppermute | solution.py:306
  35.9 9.9 %collective-permute-done.4.r4 = f32[30,8,128]{2,1,0:T(8,128)S(1)} collective-permute-done((f32[30,8,128]{2,1,0:T(8,128)S(1)}, f32[30,8,128]{2,1,0:T(8,128)S(1)}, u32[]{:S(2)}, u32[]{:S(2)}) %collective-permute-start.4) | collective-permute-done | bytes 122912 | tf_op jit(solution)/shard_map/ppermute | solution.py:306
  45.8 0.0 copy-start.5
  45.8 0.0 collective-permute-done.1.r1
  45.8 0.0 copy-start.1
  45.9 0.0 collective-permute-done.2.r2
  45.9 0.0 copy-start.2
  45.9 0.0 collective-permute-done.3.r3
  45.9 0.0 copy-start.3
  46.0 1.9 %collective-permute-start.5 = (f32[70,8,128]{2,1,0:T(8,128)S(1)}, f32[70,8,128]{2,1,0:T(8,128)S(1)}, u32[]{:S(2)}, u32[]{:S(2)}) collective-permute-start(f32[70,8,128]{2,1,0:T(8,128)S(1)} %pad_maximum_fusion), channel_id=1, source_target_pairs={{0,1},{1,0},{2,3},{3,2},{4,5},{5,4},{6,7},{7,6},{8,9},{9,8},{10,11... | collective-permute-start | bytes 860168 | tf_op jit(solution)/shard_map/ppermute | solution.py:310
  47.9 0.0 copy-done.6
  47.9 15.3 %all_to_all.22 = f32[16,1,128]{2,1,0:T(1,128)} all-to-all(f32[16,1,128]{2,1,0:T(1,128)S(1)} %bitcast.25), channel_id=1, replica_groups=mesh['patch_0'=4,'patch_1'=4,'patch_2'=16,'patch_3'=2] {'patch_2'}, dimensions={0} | all-to-all | bytes 16384 | tf_op jit(solution)/shard_map/all_to_all | solution.py:331
  63.2 1.4 %least.1 = f32[32,128]{1,0:T(8,128)} custom-call(f32[16,128]{1,0:T(8,128)} %bitcast.24), custom_call_target="tpu_custom_call" | custom-call | tf_op jit(solution)/shard_map/least/pallas_call | solution.py:122
  64.6 16.2 %all_to_all.23 = f32[32,1,128]{2,1,0:T(1,128)} all-to-all(f32[32,1,128]{2,1,0:T(1,128)} %bitcast.23), channel_id=1, replica_groups=mesh['patch_0'=4,'patch_1'=4,'patch_2'=16,'patch_3'=2] {'patch_0','patch..., dimensions={0} | all-to-all | bytes 32768 | tf_op jit(solution)/shard_map/all_to_all | solution.py:333
  80.8 0.0 collective-permute-done.5.q
  80.8 0.0 copy-start.4
  80.8 0.0 copy-done
  80.8 0.0 copy-done.5
  80.8 0.0 copy-done.1
  80.9 0.0 copy-done.2
  80.9 0.0 copy-done.3
  80.9 0.7 copy-done.4
  81.6 9.6 %advance.1 = (f32[4,1024,128]{2,1,0:T(8,128)}, f32[1,1]{1,0:T(1,128)}) custom-call(f32[4,1024,128]{2,1,0:T(8,128)} %bitcast.21, f32[1280,128]{1,0:T(8,128)} %get-tuple-element.8.rows, f32[40,8,128]{2,1,0:T(8,128)} %copy-done.1, f32[40,8,128]{2,1,0:T(8,128)} %copy-done.2, f32[40,8,128]{2,1,0:T(8,128)} %copy-done.3, f32[30,8,128]{2,1,0:T(8,128)} %copy-done.5, ...), custom_call_target="tpu_custom_call" | custom-call | tf_op jit(solution)/shard_map/advance/pallas_call | solution.py:282
  (11 shorter events, 0.1 us)
Async XLA Ops:
  4.4 43.5 %copy-start.6 = (f32[16,128]{1,0:T(8,128)S(1)}, f32[16,128]{1,0:T(8,128)}, u32[]{:S(2)}) copy-start(f32[16,128]{1,0:T(8,128)} %get-tuple-element.11) | copy-start | bytes 24580
  4.5 10.3 %collective-permute-start = (f32[90,8,128]{2,1,0:T(8,128)}, f32[90,8,128]{2,1,0:T(8,128)S(1)}, u32[]{:S(2)}, u32[]{:S(2)}) collective-permute-start(f32[90,8,128]{2,1,0:T(8,128)} %get-tuple-element.10), channel_id=1, source_target_pairs={{0,1},{1,0},{2,3},{3,2},{4,5},{5,4},{6,7},{7,6},{8,9},{9,8},{10,11... | collective-permute-start | bytes 1105928 | tf_op jit(solution)/shard_map/ppermute | solution.py:310
  14.7 66.1 %copy-start = (f32[90,8,128]{2,1,0:T(8,128)}, f32[90,8,128]{2,1,0:T(8,128)S(1)}, u32[]{:S(2)}) copy-start(f32[90,8,128]{2,1,0:T(8,128)S(1)} %collective-permute-done.w) | copy-start | bytes 1105924
  14.8 31.1 %collective-permute-start.1 = (f32[40,8,128]{2,1,0:T(8,128)S(1)}, f32[40,8,128]{2,1,0:T(8,128)S(1)}, u32[]{:S(2)}, u32[]{:S(2)}) collective-permute-start(f32[40,8,128]{2,1,0:T(8,128)S(1)} %pad_maximum_fusion.1), channel_id=1, source_target_pairs={{0,2},{1,511},{2,4},{3,1},{4,6},{5,3},{6,8},{7,5},{8,10},{9,7},{10... | collective-permute-start | bytes 491528 | tf_op jit(solution)/shard_map/ppermute | solution.py:306
  25.2 20.7 %collective-permute-start.2 = (f32[40,8,128]{2,1,0:T(8,128)S(1)}, f32[40,8,128]{2,1,0:T(8,128)S(1)}, u32[]{:S(2)}, u32[]{:S(2)}) collective-permute-start(f32[40,8,128]{2,1,0:T(8,128)S(1)} %pad_maximum_fusion.2), channel_id=1, source_target_pairs={{0,4},{1,509},{2,6},{3,511},{4,8},{5,1},{6,10},{7,3},{8,12},{9,5},... | collective-permute-start | bytes 491528 | tf_op jit(solution)/shard_map/ppermute | solution.py:306
  28.3 17.6 %collective-permute-start.3 = (f32[40,8,128]{2,1,0:T(8,128)S(1)}, f32[40,8,128]{2,1,0:T(8,128)S(1)}, u32[]{:S(2)}, u32[]{:S(2)}) collective-permute-start(f32[40,8,128]{2,1,0:T(8,128)S(1)} %pad_maximum_fusion.3), channel_id=1, source_target_pairs={{0,6},{1,507},{2,8},{3,509},{4,10},{5,511},{6,12},{7,1},{8,14},{9,... | collective-permute-start | bytes 491528 | tf_op jit(solution)/shard_map/ppermute | solution.py:306
  33.1 12.7 %collective-permute-start.4 = (f32[30,8,128]{2,1,0:T(8,128)S(1)}, f32[30,8,128]{2,1,0:T(8,128)S(1)}, u32[]{:S(2)}, u32[]{:S(2)}) collective-permute-start(f32[30,8,128]{2,1,0:T(8,128)S(1)} %pad_maximum_fusion.4), channel_id=1, source_target_pairs={{0,8},{1,505},{2,10},{3,507},{4,12},{5,509},{6,14},{7,511},{8,16},... | collective-permute-start | bytes 368648 | tf_op jit(solution)/shard_map/ppermute | solution.py:306
  45.8 35.0 %copy-start.5 = (f32[30,8,128]{2,1,0:T(8,128)}, f32[30,8,128]{2,1,0:T(8,128)S(1)}, u32[]{:S(2)}) copy-start(f32[30,8,128]{2,1,0:T(8,128)S(1)} %collective-permute-done.4.r4) | copy-start | bytes 368644
  45.8 35.0 %copy-start.1 = (f32[40,8,128]{2,1,0:T(8,128)}, f32[40,8,128]{2,1,0:T(8,128)S(1)}, u32[]{:S(2)}) copy-start(f32[40,8,128]{2,1,0:T(8,128)S(1)} %collective-permute-done.1.r1) | copy-start | bytes 491524
  45.9 35.0 %copy-start.2 = (f32[40,8,128]{2,1,0:T(8,128)}, f32[40,8,128]{2,1,0:T(8,128)S(1)}, u32[]{:S(2)}) copy-start(f32[40,8,128]{2,1,0:T(8,128)S(1)} %collective-permute-done.2.r2) | copy-start | bytes 491524
  45.9 35.0 %copy-start.3 = (f32[40,8,128]{2,1,0:T(8,128)}, f32[40,8,128]{2,1,0:T(8,128)S(1)}, u32[]{:S(2)}) copy-start(f32[40,8,128]{2,1,0:T(8,128)S(1)} %collective-permute-done.3.r3) | copy-start | bytes 491524
  46.0 34.9 %collective-permute-start.5 = (f32[70,8,128]{2,1,0:T(8,128)S(1)}, f32[70,8,128]{2,1,0:T(8,128)S(1)}, u32[]{:S(2)}, u32[]{:S(2)}) collective-permute-start(f32[70,8,128]{2,1,0:T(8,128)S(1)} %pad_maximum_fusion), channel_id=1, source_target_pairs={{0,1},{1,0},{2,3},{3,2},{4,5},{5,4},{6,7},{7,6},{8,9},{9,8},{10,11... | collective-permute-start | bytes 860168 | tf_op jit(solution)/shard_map/ppermute | solution.py:310
  80.8 0.7 copy-start.4

commit v2 on v1

v2 whole, which is shorter than its diff:
```python
import jax
import jax.numpy as jnp
from jax import lax
from jax.experimental import pallas as pl
from jax.experimental.pallas import tpu as pltpu
from jax.sharding import Mesh
from jax.sharding import PartitionSpec as P

AXES = ("patch_0", "patch_1", "patch_2", "patch_3")
SHAPE = (4, 4, 16, 2)
COURANT = 0.4
CHUNKS = 8
NEAR = 64
ROWS = 80
PACK = 16 * ROWS
DEEP = 2 * 4 * 2 * 32
T = PACK // 128
LINE = 36
SPAN = 1160
F32 = jnp.float32
VMEM = pl.BlockSpec(memory_space=pltpu.VMEM)
ANY = pl.BlockSpec(memory_space=pl.ANY)


def spacing_of(level):
    return jnp.where(level == 6, 1.0, jnp.where(level == 5, 2.0, 4.0)).astype(F32)


def start_chunks(source, target, sems, inward=True):
    width = 1024 // CHUNKS
    copies = []
    for chunk in range(CHUNKS):
        part = pl.ds(chunk * width, width)
        copies.append(pltpu.make_async_copy(source.at[:, part], target.at[:, part], sems.at[chunk]))
        if inward:
            copies[-1].start()
    return copies


def core_index():
    return lax.axis_index("patch_3")


def pack_kernel(fields, level, send, own, swap, rows, deep, cells, sems):
    copies = start_chunks(fields, cells, sems)
    width = 32 // CHUNKS
    fastest = jnp.zeros((32, 128), F32)
    for chunk in range(CHUNKS):
        copies[chunk].wait()

        def speeds(x, best):
            h, m, n = [cells[c, pl.ds(pl.multiple_of(32 * x, 32), 32), :] for c in range(3)]
            v = jnp.maximum(jnp.abs(m), jnp.abs(n)) / h
            return jnp.maximum(best, v + jnp.sqrt(h))

        fastest = lax.fori_loop(chunk * width, (chunk + 1) * width, speeds, fastest, unroll=True)
    top = jnp.max(fastest, axis=0, keepdims=True)
    ratio = spacing_of(level[...]) / top
    swap[9 * T] = jnp.broadcast_to(jnp.min(ratio, axis=1, keepdims=True), (8, 128))

    for face in range(4):
        for c in range(4):
            base = (face * 4 + c) * ROWS
            at = [k if face % 2 == 0 else 31 - k for k in range(4)]
            inner = ((face - 2) * 4 + c) * 64
            for k in range(4):
                if face < 2 and k < 2:
                    rows[pl.ds(base + 32 * k, 32), :] = cells[c, pl.ds(32 * at[k], 32), :]
                if face >= 2:
                    line = cells[c, pl.ds(at[k], 32, stride=32), :]
                    if k < 2:
                        rows[pl.ds(base + 32 * k, 32), :] = line
                    else:
                        deep[pl.ds(inner + 32 * (k - 2), 32), :] = line

            def take(k, odd):
                if face < 2:
                    return cells[c, pl.ds(at[k] * 32 + odd, 16, stride=2), :]
                return deep[pl.ds(inner + 32 * (k - 2) + odd, 16, stride=2), :]

            total = take(2, 0) + take(3, 0)
            total = total + take(2, 1)
            total = total + take(3, 1)
            rows[pl.ds(base + NEAR, 16), :] = 0.25 * total

    lane = lax.broadcasted_iota(jnp.int32, (16, 128), 1)
    block = lax.broadcasted_iota(jnp.int32, (16, 128), 0)
    spread = jnp.where(((lane // 8) ^ (8 * core_index())) == block, 1.0, 0.0).astype(F32)
    listed = jnp.dot(send[...].astype(F32), spread, preferred_element_type=F32)
    slot = lax.broadcasted_iota(jnp.int32, (8, 128), 0)
    mine = (lax.broadcasted_iota(jnp.int32, (8, 128), 1) % 8) == slot
    chosen = jnp.sum(jnp.where(mine, listed, 0.0), axis=0, keepdims=True).astype(jnp.int32)
    index = jnp.broadcast_to(chosen, (128, 128))
    for tile in range(T):
        picked = jnp.take_along_axis(rows[pl.ds(tile * 128, 128), :], index, axis=1)
        turned = picked.T
        swap[8 * T + tile] = turned[0:8]
        for j in range(1, 8):
            own[(j - 1) * T + tile] = turned[8 * j : 8 * j + 8]
        for j in range(8):
            swap[j * T + tile] = turned[64 + 8 * j : 72 + 8 * j]


def tiles(n):
    return jax.ShapeDtypeStruct((n, 8, 128), F32)


def pack(fields, level, send):
    return pl.pallas_call(
        pack_kernel,
        out_shape=(
            tiles(7 * T),
            tiles(9 * T + 1),
            jax.ShapeDtypeStruct((PACK, 128), F32),
            jax.ShapeDtypeStruct((DEEP, 128), F32),
        ),
        in_specs=[ANY, VMEM, VMEM],
        out_specs=(VMEM,) * 4,
        scratch_shapes=[pltpu.VMEM((4, 1024, 128), F32), pltpu.SemaphoreType.DMA((CHUNKS,))],
        name="pack",
    )(fields, level, send)


def physical(q, normal):
    h = q[0]
    m = q[normal]
    v = m / h
    flux = [m, q[1] * v, q[2] * v, q[3] * v]
    flux[normal] = flux[normal] + 0.5 * h * h
    return flux, jnp.abs(v) + jnp.sqrt(h)


def interface(left, right, normal):
    lf, ls = physical(left, normal)
    rf, rs = physical(right, normal)
    widest = 0.5 * jnp.maximum(ls, rs)
    return [0.5 * (lf[c] + rf[c]) - widest * (right[c] - left[c]) for c in range(4)]


def inner_kernel(fields, out, cells, lines, fluxes, sems):
    copies = start_chunks(fields, cells, sems)
    width = 32 // CHUNKS

    def lay(x, carry):
        for c in range(4):
            line = cells[c, pl.ds(pl.multiple_of(32 * x, 32), 32), :]
            lines[pl.ds(c * SPAN + x * LINE + 2, 32), :] = line
        return carry

    for chunk in range(CHUNKS):
        copies[chunk].wait()
        lax.fori_loop(chunk * width, (chunk + 1) * width, lay, 0, unroll=True)

    def along_y(n, carry):
        r = 1 + 8 * n
        left, right = [], []
        for c in range(4):
            before, here, after, beyond = [
                lines[pl.ds(c * SPAN + r + d, 8), :] for d in (-1, 0, 1, 2)
            ]
            left.append(here + 0.25 * (after - before))
            right.append(after - 0.25 * (beyond - here))
        flux = interface(left, right, 2)
        for c in range(4):
            fluxes[pl.ds(c * SPAN + r, 8), :] = flux[c]
        return carry

    lax.fori_loop(0, 144, along_y, 0, unroll=4)

    sub = lax.broadcasted_iota(jnp.int32, (8, 128), 0)
    for part in range(4):
        y = 8 * part

        def load(x):
            return [cells[c, pl.ds(pl.multiple_of(32 * x + y, 8), 8), :] for c in range(4)]

        def across(c, x):
            at = c * SPAN + x * LINE + y
            change = fluxes[pl.ds(at + 2, 8), :] - fluxes[pl.ds(at + 1, 8), :]
            if part == 0:
                change = jnp.where(sub >= 2, change, 0.0)
            if part == 3:
                change = jnp.where(sub < 6, change, 0.0)
            return change

        def store(c, x, value):
            out[c, pl.ds(pl.multiple_of(32 * x + y, 8), 8), :] = value

        def along_x(x, carry):
            here, ahead, left, last = carry
            beyond = load(x + 2)
            lean = [0.25 * (beyond[c] - here[c]) for c in range(4)]
            right = [ahead[c] - lean[c] for c in range(4)]
            flux = interface(left, right, 1)
            if last is not None:
                for c in range(4):
                    store(c, x, (flux[c] - last[c]) + across(c, x))
            return ahead, beyond, [ahead[c] + lean[c] for c in range(4)], flux

        first, second, third = load(0), load(1), load(2)
        left = [second[c] + 0.25 * (third[c] - first[c]) for c in range(4)]
        state = along_x(1, (second, third, left, None))
        lax.fori_loop(2, 30, along_x, state, unroll=4)
        for x in (0, 1, 30, 31):
            for c in range(4):
                store(c, x, across(c, x))


def inner(fields):
    return pl.pallas_call(
        inner_kernel,
        out_shape=jax.ShapeDtypeStruct((4, 1024, 128), F32),
        in_specs=[ANY],
        out_specs=VMEM,
        scratch_shapes=[
            pltpu.VMEM((4, 1024, 128), F32),
            pltpu.VMEM((4 * SPAN, 128), F32),
            pltpu.VMEM((4 * SPAN, 128), F32),
            pltpu.SemaphoreType.DMA((CHUNKS,)),
        ],
        name="inner",
    )(fields)


def step_kernel(
    fields, inside, rows, deep, r1, r2, r3, r4, w, q, got, level, relation, half, refs,
    out, step, cells, change, fresh, ghosts, pool, edge, weave, in_sems, change_sems, out_sems,
):
    field_copies = start_chunks(fields, cells, in_sems)
    change_copies = start_chunks(inside, change, change_sems)
    sources = [
        (r1, T), (r1, 0), (r2, T), (r2, 0), (r3, T), (r3, 0), (r4, T), (r4, 0),
        (w, 8 * T), (q, T), (q, 0), (q, 3 * T), (q, 2 * T), (q, 5 * T), (q, 4 * T), (q, 6 * T),
    ]
    for tile in range(T):
        joined = jnp.concatenate([ref[at + tile] for ref, at in sources], axis=0)
        pool[pl.ds(tile * 128, 128), :] = joined.T

    flip = 64 * core_index()
    for face in range(4):
        kind = relation[pl.ds(face, 1), :]
        upper = half[pl.ds(face, 1), :] == 1
        names = [refs[pl.ds(2 * face + m, 1), :] for m in range(2)]
        away = [name >= 128 for name in names]
        local = [name & 127 for name in names]
        remote = [(name & 127) ^ flip for name in names]

        def gather(own_rows, pool_rows, m):
            shape = own_rows.shape
            a = jnp.take_along_axis(own_rows, jnp.broadcast_to(local[m], shape), axis=1)
            b = jnp.take_along_axis(pool_rows, jnp.broadcast_to(remote[m], shape), axis=1)
            return jnp.where(away[m], b, a)

        for c in range(4):
            base = ((face ^ 1) * 4 + c) * ROWS

            def coarse_first(ref):
                total = ref[pl.ds(base, 16, stride=2), :] + ref[pl.ds(base + 32, 16, stride=2), :]
                total = total + ref[pl.ds(base + 1, 16, stride=2), :]
                total = total + ref[pl.ds(base + 33, 16, stride=2), :]
                return 0.25 * total

            near = gather(rows[pl.ds(base, NEAR), :], pool[pl.ds(base, NEAR), :], 0)
            pairs = [
                (coarse_first(rows), coarse_first(pool)),
                (rows[pl.ds(base + NEAR, 16), :], pool[pl.ds(base + NEAR, 16), :]),
            ]
            column = near[0:32]
            spot = 40 * (4 * face + c)
            edge[pl.ds(spot + 1, 32), :] = column
            edge[pl.ds(spot, 1), :] = column[0:1]
            edge[pl.ds(spot + 33, 1), :] = column[31:32]
            slope = edge[pl.ds(spot + 2, 32), :] - edge[pl.ds(spot, 32), :]
            value = jnp.where(upper, column[16:32], column[0:16])
            tilt = 0.125 * jnp.where(upper, slope[16:32], slope[0:16])
            turn = 32 * (4 * face + c)
            weave[pl.ds(turn, 16, stride=2), :] = value - tilt
            weave[pl.ds(turn + 1, 16, stride=2), :] = value + tilt
            coarse = weave[pl.ds(turn, 32), :]
            sign = -1.0 if c == 1 + face // 2 else 1.0
            for g in range(2):
                fine = jnp.concatenate([gather(*pairs[g], 0), gather(*pairs[g], 1)], axis=0)
                mirror = sign * rows[pl.ds((face * 4 + c) * ROWS + 32 * g, 32), :]
                ghosts[pl.ds(((face * 4 + c) * 2 + g) * 32, 32), :] = jnp.where(
                    kind == 0,
                    mirror,
                    jnp.where(
                        kind == 1,
                        near[32 * g : 32 * g + 32],
                        jnp.where(kind == 2, coarse, fine),
                    ),
                )

    for copy in field_copies + change_copies:
        copy.wait()

    for face in range(4):

        def border(j, carry):
            def part(c, depth):
                along = pl.multiple_of(8 * j, 8)
                if depth < 0:
                    return ghosts[pl.ds(((face * 4 + c) * 2 - depth - 1) * 32 + along, 8), :]
                if face < 2:
                    x = depth if face == 0 else 31 - depth
                    return cells[c, pl.ds(32 * x + along, 8), :]
                if depth < 2:
                    return rows[pl.ds((face * 4 + c) * ROWS + 32 * depth + along, 8), :]
                return deep[pl.ds(((face - 2) * 4 + c) * 64 + 32 * (depth - 2) + along, 8), :]

            depths = [-2, -1, 0, 1, 2, 3]
            if face % 2 == 1:
                depths = depths[::-1]
            q6 = [[part(c, depth) for c in range(4)] for depth in depths]
            lean = [[0.25 * (q6[i + 1][c] - q6[i - 1][c]) for c in range(4)] for i in range(1, 5)]
            flux = []
            for i in range(1, 4):
                left = [q6[i][c] + lean[i - 1][c] for c in range(4)]
                right = [q6[i + 1][c] - lean[i][c] for c in range(4)]
                flux.append(interface(left, right, 1 + face // 2))
            for i in range(2):
                depth = depths[i + 2]
                where = depth if face % 2 == 0 else 31 - depth
                for c in range(4):
                    extra = flux[i + 1][c] - flux[i][c]
                    if face < 2:
                        spot = pl.ds(pl.multiple_of(32 * where + 8 * j, 8), 8)
                    else:
                        spot = pl.ds(256 * j + where, 8, stride=32)
                    change[c, spot, :] = change[c, spot, :] + extra
            return carry

        lax.fori_loop(0, 4, border, 0, unroll=2)

    low = jnp.min(jnp.min(got[...], axis=0, keepdims=True), axis=1, keepdims=True)
    chosen = COURANT * low
    step[...] = chosen
    ratio = chosen / spacing_of(level[...])

    out_copies = start_chunks(fresh, out, out_sems, inward=False)
    width = 1024 // CHUNKS
    for chunk in range(CHUNKS):

        def update(n, carry):
            spot = pl.ds(pl.multiple_of(chunk * width + 32 * n, 32), 32)
            for c in range(4):
                fresh[c, spot, :] = cells[c, spot, :] - ratio * change[c, spot, :]
            return carry

        lax.fori_loop(0, width // 32, update, 0, unroll=True)
        out_copies[chunk].start()
    for copy in out_copies:
        copy.wait()


def advance(*operands):
    return pl.pallas_call(
        step_kernel,
        out_shape=(
            jax.ShapeDtypeStruct((4, 1024, 128), F32),
            jax.ShapeDtypeStruct((1, 1), F32),
        ),
        in_specs=[ANY] * 2 + [VMEM] * 13,
        out_specs=(ANY, VMEM),
        scratch_shapes=[
            pltpu.VMEM((4, 1024, 128), F32),
            pltpu.VMEM((4, 1024, 128), F32),
            pltpu.VMEM((4, 1024, 128), F32),
            pltpu.VMEM((16 * 2 * 32, 128), F32),
            pltpu.VMEM((PACK, 128), F32),
            pltpu.VMEM((16 * 40, 128), F32),
            pltpu.VMEM((16 * 32, 128), F32),
            pltpu.SemaphoreType.DMA((CHUNKS,)),
            pltpu.SemaphoreType.DMA((CHUNKS,)),
            pltpu.SemaphoreType.DMA((CHUNKS,)),
        ],
        name="advance",
    )(*operands)


def two_way(array, chips):
    n = lax.axis_size(AXES)
    pairs = [(i, (i + (2 * chips if i % 2 == 0 else -2 * chips)) % n) for i in range(n)]
    return lax.ppermute(array, AXES, pairs)


def swap_cores(array):
    return lax.ppermute(array, AXES, [(i, i ^ 1) for i in range(lax.axis_size(AXES))])


def cross(array):
    n = lax.axis_size(AXES)
    return lax.ppermute(array, AXES, [(i, (i + (-3 if i % 2 else 3)) % n) for i in range(n)])


def compute(fields, patch_level, relation, face_half, neighbour, send_list):
    level = patch_level.reshape(1, 128)
    flat = fields.reshape(4, 1024, 128)
    own, swap, rows, deep = pack(flat, level, send_list[0].T)
    w = swap_cores(swap)

    def blk(array, n, count=1):
        return array[n * T : (n + count) * T]

    def ahead(j):
        return blk(own, j - 2)

    def beside(j):
        return blk(w, j - 1)

    low = jnp.minimum(swap[9 * T :], w[9 * T :])
    r4 = two_way(jnp.concatenate([ahead(8), beside(7), low]), 4)
    inside = inner(flat)
    low = jnp.minimum(low, r4[2 * T :])
    r3 = two_way(jnp.concatenate([ahead(6), beside(5), beside(8), low]), 3)
    r2 = two_way(jnp.concatenate([ahead(4), beside(3), ahead(7), beside(6), low]), 2)
    r1 = two_way(jnp.concatenate([ahead(2), beside(1), ahead(5), beside(4), low]), 1)
    q = cross(
        jnp.concatenate([ahead(3), beside(2), blk(r1, 2, 2), blk(r2, 2, 2), blk(r3, 2)])
    )
    depth = lax.axis_size("patch_2")
    columns = lax.axis_size(("patch_0", "patch_1"))
    low = jnp.minimum(jnp.minimum(low, r1[4 * T :]), jnp.minimum(r2[4 * T :], r3[3 * T :]))
    least = jnp.broadcast_to(low[0, :1], (2 * columns, 128))
    groups = [
        [(r * depth + (g + c) % depth) * 2 + c for r in range(columns) for c in range(2)]
        for g in range(depth)
    ]
    got = lax.all_to_all(least, AXES, 0, 0, tiled=True, axis_index_groups=groups)
    advanced, step = advance(
        flat, inside, rows, deep, r1, r2, r3, r4, w, q, got, level, relation.T, face_half.T,
        neighbour.transpose(1, 2, 0).reshape(8, 128),
    )
    return advanced.reshape(fields.shape), step[0, 0]


def stepper(mesh):
    split = Mesh(mesh.devices.reshape(SHAPE), AXES)
    return jax.shard_map(
        compute,
        mesh=split,
        in_specs=(
            P(None, None, None, AXES),
            P(AXES),
            P(AXES, None),
            P(AXES, None),
            P(AXES, None, None),
            P(AXES, None, None),
        ),
        out_specs=(P(None, None, None, AXES), P()),
        check_vma=False,
    )


def solution(mesh):
    return stepper(mesh)
```

time: 91.7 us -> 81.9 us (0.89)
  blocking collectives: 31.5 us -> 0 us
  starting transfers between devices: 31.7 us -> 47.6 us
  Pallas kernels: 14.7 us -> 17.2 us
  local copies, waits for them, and re-layouts: 1.68 us -> 3.21 us
  waiting for transfers between devices: 10.5 us -> 11.7 us
    all_to_all x2 -> x0, blocking collectives: 31.5 us -> none  [the longest x1 16.2 us: on_device(): lax.all_to_all(spread_least(got, lax.axis_size(others)), others, 0, 0, ti...]
    all_to_all x0 -> x1, starting transfers between devices: none -> 7.5 us  [compute(): lax.all_to_all(least, AXES, 0, 0, tiled=True, axis_index_groups=groups)]
    ppermute x4, starting transfers between devices: 21 us -> 27.8 us  [two_way(): return lax.ppermute(array, AXES, pairs)]
    pallas_call x2, Pallas kernels: 5.19 us -> 10.4 us  [the longest x1 6.33 us: inner(): pl.pallas_call(inner_kernel, out_shape=jax.ShapeDtypeStruct((4, 1024, 128...]
    ppermute x0 -> x1, starting transfers between devices: none -> 3.57 us  [cross(): lax.ppermute(array, AXES, [(i, (i + (-3 if i % 2 else 3)) % n) for i in r...]
    pallas_call x1, Pallas kernels: 9.55 us -> 6.74 us  [advance(): pl.pallas_call(step_kernel, out_shape=(jax.ShapeDtypeStruct((4, 1024, 128...]
    ppermute x2 -> x1, starting transfers between devices: 10.7 us -> 8.75 us  [swap_cores(): lax.ppermute(array, AXES, [(i, i ^ 1) for i in range(lax.axis_size(AXES))])]
    unnamed x14 -> x20, local copies, waits for them, and re-layouts: 0.71 us -> 2.59 us
  transfers between devices with their start and end apart: 6 -> 7, of which waited for: 2 -> 4; matrix products, arithmetic and copies ran while one was open for 1% -> 2% of each run, Pallas kernels for 2% -> 8%
where the time goes in v2:
time: 81.9 us; the launch traced here: 81.3 us
  starting transfers between devices  47.6 us (58%)
  Pallas kernels  17.2 us (21%)
  waiting for transfers between devices  11.7 us (14%)
  local copies, waits for them, and re-layouts  3.21 us (4%)
  between operations  0.84 us (1%)
    ppermute x4, starting transfers between devices, two_way(): return lax.ppermute(array, AXES, pairs)  27.8 us
    ppermute x4, waiting for transfers between devices, two_way(): return lax.ppermute(array, AXES, pairs)  10.6 us
    ppermute x1, starting transfers between devices, swap_cores(): lax.ppermute(array, AXES, [(i, i ^ 1) for i in range(lax.axis_size(AXES))])  8.75 us
    all_to_all x1, starting transfers between devices, compute(): lax.all_to_all(least, AXES, 0, 0, tiled=True, axis_index_groups=groups)  7.5 us
    pallas_call x1, Pallas kernels, advance(): pl.pallas_call(step_kernel, out_shape=(jax.ShapeDtypeStruct((4, 1024, 128...  6.74 us
    pallas_call x1, Pallas kernels, inner(): pl.pallas_call(inner_kernel, out_shape=jax.ShapeDtypeStruct((4, 1024, 128...  6.33 us
    pallas_call x1, Pallas kernels, pack(): pl.pallas_call(pack_kernel, out_shape=(tiles(7 * T), tiles(9 * T + 1), ja...  4.1 us
    ppermute x1, starting transfers between devices, cross(): lax.ppermute(array, AXES, [(i, (i + (-3 if i % 2 else 3)) % n) for i in r...  3.57 us
  transfers between devices with their start and end apart: 7, of which 4 were waited for; matrix products, arithmetic and copies ran while one was open for 2% of the time, Pallas kernels for 8%

profile of v2, /device:TPU:1, one launch (start us, length us, event | category | flops | bytes accessed | tf_op | source)
XLA Modules:
  0.0 81.3 jit_solution(7290710161857834141)
XLA Ops:
  0.6 4.1 %pack.1 = (f32[70,8,128]{2,1,0:T(8,128)}, f32[91,8,128]{2,1,0:T(8,128)}, f32[1280,128]{1,0:T(8,128)}, f32[512,128]{1,0:T(8,128)}) custom-call(f32[4,1024,128]{2,1,0:T(8,128)} %bitcast.15, s32[1,128]{1,0:T(1,128)} %bitcast.23, s32[8,16]{1,0:T(8,128)} %bitcast.19), custom_call_target="tpu_custom_call" | custom-call | tf_op jit(solution)/shard_map/pack/pallas_call | solution.py:109
  4.7 8.7 %collective-permute-start = (f32[91,8,128]{2,1,0:T(8,128)}, f32[91,8,128]{2,1,0:T(8,128)S(1)}, u32[]{:S(2)}, u32[]{:S(2)}) collective-permute-start(f32[91,8,128]{2,1,0:T(8,128)} %get-tuple-element.11), channel_id=1, source_target_pairs={{0,1},{1,0},{2,3},{3,2},{4,5},{5,4},{6,7},{7,6},{8,9},{9,8},{10,11... | collective-permute-start | bytes 1118216 | tf_op jit(solution)/shard_map/ppermute | solution.py:388
  13.5 0.8 slice_dynamic-update-slice_fusion.10
  14.3 0.7 collective-permute-done.w
  15.0 0.0 copy-start
  15.0 1.0 %slice_dynamic-update-slice_fusion.8 = (f32[70,8,128]{2,1,0:T(8,128)S(1)}, f32[10,8,128]{2,1,0:T(8,128)S(1)}, f32[41,8,128]{2,1,0:T(8,128)S(1)}, f32[10,8,128]{2,1,0:T(8,128)S(1)}, f32[41,8,128]{2,1,0:T(8,128)S(1)}) fusion(f32[70,8,128]{2,1,0:T(8,128)} %get-tuple-element.10, f32[41,8,128]{2,1,0:T(8,128)S(1)} %get-tuple-element.22, ...), kind=kLoop, calls=%fused_computation.10 | loop fusion | bytes 409600
  16.0 0.7 slice_minimum_fusion.3
  16.8 11.8 %collective-permute-start.1 = (f32[21,8,128]{2,1,0:T(8,128)S(1)}, f32[21,8,128]{2,1,0:T(8,128)S(1)}, u32[]{:S(2)}, u32[]{:S(2)}) collective-permute-start(f32[21,8,128]{2,1,0:T(8,128)S(1)} %pad_maximum_fusion.1), channel_id=1, source_target_pairs={{0,8},{1,505},{2,10},{3,507},{4,12},{5,509},{6,14},{7,511},{8,16},... | collective-permute-start | bytes 258056 | tf_op jit(solution)/shard_map/ppermute | solution.py:384
  28.5 4.2 %collective-permute-done.1.r4 = f32[21,8,128]{2,1,0:T(8,128)S(1)} collective-permute-done((f32[21,8,128]{2,1,0:T(8,128)S(1)}, f32[21,8,128]{2,1,0:T(8,128)S(1)}, u32[]{:S(2)}, u32[]{:S(2)}) %collective-permute-start.1) | collective-permute-done | bytes 86048 | tf_op jit(solution)/shard_map/ppermute | solution.py:384
  32.7 0.0 copy-start.5
  32.7 8.1 %collective-permute-start.2 = (f32[41,8,128]{2,1,0:T(8,128)S(1)}, f32[41,8,128]{2,1,0:T(8,128)S(1)}, u32[]{:S(2)}, u32[]{:S(2)}) collective-permute-start(f32[41,8,128]{2,1,0:T(8,128)S(1)} %constant_dynamic-update-slice_fusion), channel_id=1, source_target_pairs={{0,2},{1,511},{2,4},{3,1},{4,6},{5,3},{6,8},{7,5},{8,10},{9,7},{10... | collective-permute-start | bytes 503816 | tf_op jit(solution)/shard_map/ppermute | solution.py:384
  40.9 6.0 %collective-permute-start.4 = (f32[31,8,128]{2,1,0:T(8,128)S(1)}, f32[31,8,128]{2,1,0:T(8,128)S(1)}, u32[]{:S(2)}, u32[]{:S(2)}) collective-permute-start(f32[31,8,128]{2,1,0:T(8,128)S(1)} %pad_maximum_fusion), channel_id=1, source_target_pairs={{0,6},{1,507},{2,8},{3,509},{4,10},{5,511},{6,12},{7,1},{8,14},{9,... | collective-permute-start | bytes 380936 | tf_op jit(solution)/shard_map/ppermute | solution.py:384
  46.9 1.9 %collective-permute-start.3 = (f32[41,8,128]{2,1,0:T(8,128)S(1)}, f32[41,8,128]{2,1,0:T(8,128)S(1)}, u32[]{:S(2)}, u32[]{:S(2)}) collective-permute-start(f32[41,8,128]{2,1,0:T(8,128)S(1)} %get-tuple-element.14), channel_id=1, source_target_pairs={{0,4},{1,509},{2,6},{3,511},{4,8},{5,1},{6,10},{7,3},{8,12},{9,5},... | collective-permute-start | bytes 503816 | tf_op jit(solution)/shard_map/ppermute | solution.py:384
  48.8 0.0 collective-permute-done.2.r1
  48.8 0.0 copy-start.1
  48.8 6.5 %collective-permute-done.3.r2 = f32[41,8,128]{2,1,0:T(8,128)S(1)} collective-permute-done((f32[41,8,128]{2,1,0:T(8,128)S(1)}, f32[41,8,128]{2,1,0:T(8,128)S(1)}, u32[]{:S(2)}, u32[]{:S(2)}) %collective-permute-start.3) | collective-permute-done | bytes 167968 | tf_op jit(solution)/shard_map/ppermute | solution.py:384
  55.3 0.0 copy-start.2
  55.3 0.0 collective-permute-done.4.r3
  55.3 0.0 copy-start.4
  55.3 3.6 %collective-permute-start.5 = (f32[70,8,128]{2,1,0:T(8,128)S(1)}, f32[70,8,128]{2,1,0:T(8,128)S(1)}, u32[]{:S(2)}, u32[]{:S(2)}) collective-permute-start(f32[70,8,128]{2,1,0:T(8,128)S(1)} %slice_dynamic-update-slice_fusion.2), channel_id=1, source_target_pairs={{0,3},{1,510},{2,5},{3,0},{4,7},{5,2},{6,9},{7,4},{8,11},{9,6},{10... | collective-permute-start | bytes 860168 | tf_op jit(solution)/shard_map/ppermute | solution.py:393
  58.9 0.6 broadcast_in_dim.2
  59.6 7.5 %all-to-all-start = ((f32[32,1,128]{2,1,0:T(1,128)}), f32[32,1,128]{2,1,0:T(1,128)S(1)}, u32[]{:S(2)}, u32[]{:S(2)}) async-start(f32[32,1,128]{2,1,0:T(1,128)} %broadcast_in_dim.2), calls=%async_computation | async-start | bytes 32768 | tf_op jit(solution)/shard_map/all_to_all | solution.py:429
  67.1 6.3 %inner.1.inside = f32[4,1024,128]{2,1,0:T(8,128)} custom-call(f32[4,1024,128]{2,1,0:T(8,128)} %bitcast.16), custom_call_target="tpu_custom_call" | custom-call | tf_op jit(solution)/shard_map/inner/pallas_call | solution.py:210
  73.4 0.0 copy-done
  73.4 0.0 copy-done.5
  73.4 0.0 copy-done.1
  73.4 0.0 copy-done.2
  73.5 0.0 copy-done.4
  73.5 0.3 all-to-all-done
  73.8 0.0 copy-start.6
  73.8 0.0 collective-permute-done.5.q
  73.8 0.0 copy-start.3
  73.8 0.6 copy-done.6
  74.4 0.1 copy-done.3
  74.5 6.7 %advance.1 = (f32[4,1024,128]{2,1,0:T(8,128)}, f32[1,1]{1,0:T(1,128)}) custom-call(f32[4,1024,128]{2,1,0:T(8,128)} %bitcast.17, f32[4,1024,128]{2,1,0:T(8,128)} %inner.1.inside, f32[1280,128]{1,0:T(8,128)} %get-tuple-element.8.rows, f32[512,128]{1,0:T(8,128)} %get-tuple-element.9.deep, f32[41,8,128]{2,1,0:T(8,128)} %copy-done.1, f32[41,8,128]{2,1,0:T(8,128)} %copy-done.2, ...), custom_call_target="tpu_custom_call" | custom-call | tf_op jit(solution)/shard_map/advance/pallas_call | solution.py:357
  (11 shorter events, 0.1 us)
Async XLA Ops:
  4.7 10.3 %collective-permute-start = (f32[91,8,128]{2,1,0:T(8,128)}, f32[91,8,128]{2,1,0:T(8,128)S(1)}, u32[]{:S(2)}, u32[]{:S(2)}) collective-permute-start(f32[91,8,128]{2,1,0:T(8,128)} %get-tuple-element.11), channel_id=1, source_target_pairs={{0,1},{1,0},{2,3},{3,2},{4,5},{5,4},{6,7},{7,6},{8,9},{9,8},{10,11... | collective-permute-start | bytes 1118216 | tf_op jit(solution)/shard_map/ppermute | solution.py:388
  15.0 58.4 %copy-start = (f32[91,8,128]{2,1,0:T(8,128)}, f32[91,8,128]{2,1,0:T(8,128)S(1)}, u32[]{:S(2)}) copy-start(f32[91,8,128]{2,1,0:T(8,128)S(1)} %collective-permute-done.w) | copy-start | bytes 1118212
  16.8 15.9 %collective-permute-start.1 = (f32[21,8,128]{2,1,0:T(8,128)S(1)}, f32[21,8,128]{2,1,0:T(8,128)S(1)}, u32[]{:S(2)}, u32[]{:S(2)}) collective-permute-start(f32[21,8,128]{2,1,0:T(8,128)S(1)} %pad_maximum_fusion.1), channel_id=1, source_target_pairs={{0,8},{1,505},{2,10},{3,507},{4,12},{5,509},{6,14},{7,511},{8,16},... | collective-permute-start | bytes 258056 | tf_op jit(solution)/shard_map/ppermute | solution.py:384
  32.7 40.7 %copy-start.5 = (f32[21,8,128]{2,1,0:T(8,128)}, f32[21,8,128]{2,1,0:T(8,128)S(1)}, u32[]{:S(2)}) copy-start(f32[21,8,128]{2,1,0:T(8,128)S(1)} %collective-permute-done.1.r4) | copy-start | bytes 258052
  32.7 16.1 %collective-permute-start.2 = (f32[41,8,128]{2,1,0:T(8,128)S(1)}, f32[41,8,128]{2,1,0:T(8,128)S(1)}, u32[]{:S(2)}, u32[]{:S(2)}) collective-permute-start(f32[41,8,128]{2,1,0:T(8,128)S(1)} %constant_dynamic-update-slice_fusion), channel_id=1, source_target_pairs={{0,2},{1,511},{2,4},{3,1},{4,6},{5,3},{6,8},{7,5},{8,10},{9,7},{10... | collective-permute-start | bytes 503816 | tf_op jit(solution)/shard_map/ppermute | solution.py:384
  40.9 14.5 %collective-permute-start.4 = (f32[31,8,128]{2,1,0:T(8,128)S(1)}, f32[31,8,128]{2,1,0:T(8,128)S(1)}, u32[]{:S(2)}, u32[]{:S(2)}) collective-permute-start(f32[31,8,128]{2,1,0:T(8,128)S(1)} %pad_maximum_fusion), channel_id=1, source_target_pairs={{0,6},{1,507},{2,8},{3,509},{4,10},{5,511},{6,12},{7,1},{8,14},{9,... | collective-permute-start | bytes 380936 | tf_op jit(solution)/shard_map/ppermute | solution.py:384
  46.9 8.4 %collective-permute-start.3 = (f32[41,8,128]{2,1,0:T(8,128)S(1)}, f32[41,8,128]{2,1,0:T(8,128)S(1)}, u32[]{:S(2)}, u32[]{:S(2)}) collective-permute-start(f32[41,8,128]{2,1,0:T(8,128)S(1)} %get-tuple-element.14), channel_id=1, source_target_pairs={{0,4},{1,509},{2,6},{3,511},{4,8},{5,1},{6,10},{7,3},{8,12},{9,5},... | collective-permute-start | bytes 503816 | tf_op jit(solution)/shard_map/ppermute | solution.py:384
  48.8 24.6 %copy-start.1 = (f32[41,8,128]{2,1,0:T(8,128)}, f32[41,8,128]{2,1,0:T(8,128)S(1)}, u32[]{:S(2)}) copy-start(f32[41,8,128]{2,1,0:T(8,128)S(1)} %collective-permute-done.2.r1) | copy-start | bytes 503812
  55.3 18.1 %copy-start.2 = (f32[41,8,128]{2,1,0:T(8,128)}, f32[41,8,128]{2,1,0:T(8,128)S(1)}, u32[]{:S(2)}) copy-start(f32[41,8,128]{2,1,0:T(8,128)S(1)} %collective-permute-done.3.r2) | copy-start | bytes 503812
  55.3 18.1 %copy-start.4 = (f32[31,8,128]{2,1,0:T(8,128)}, f32[31,8,128]{2,1,0:T(8,128)S(1)}, u32[]{:S(2)}) copy-start(f32[31,8,128]{2,1,0:T(8,128)S(1)} %collective-permute-done.4.r3) | copy-start | bytes 380932
  55.3 18.5 %collective-permute-start.5 = (f32[70,8,128]{2,1,0:T(8,128)S(1)}, f32[70,8,128]{2,1,0:T(8,128)S(1)}, u32[]{:S(2)}, u32[]{:S(2)}) collective-permute-start(f32[70,8,128]{2,1,0:T(8,128)S(1)} %slice_dynamic-update-slice_fusion.2), channel_id=1, source_target_pairs={{0,3},{1,510},{2,5},{3,0},{4,7},{5,2},{6,9},{7,4},{8,11},{9,6},{10... | collective-permute-start | bytes 860168 | tf_op jit(solution)/shard_map/ppermute | solution.py:393
  59.6 14.2 %all-to-all-start = ((f32[32,1,128]{2,1,0:T(1,128)}), f32[32,1,128]{2,1,0:T(1,128)S(1)}, u32[]{:S(2)}, u32[]{:S(2)}) async-start(f32[32,1,128]{2,1,0:T(1,128)} %broadcast_in_dim.2), calls=%async_computation | async-start | bytes 32768 | tf_op jit(solution)/shard_map/all_to_all | solution.py:429
  73.8 0.6 copy-start.6
  73.8 0.7 copy-start.3

commit v3 on v2

--- a/solution.py
+++ b/solution.py
@@ -26,14 +26,13 @@
     return jnp.where(level == 6, 1.0, jnp.where(level == 5, 2.0, 4.0)).astype(F32)
 
 
-def start_chunks(source, target, sems, inward=True):
+def start_chunks(source, target, sems):
     width = 1024 // CHUNKS
     copies = []
     for chunk in range(CHUNKS):
         part = pl.ds(chunk * width, width)
         copies.append(pltpu.make_async_copy(source.at[:, part], target.at[:, part], sems.at[chunk]))
-        if inward:
-            copies[-1].start()
+        copies[-1].start()
     return copies
 
 
@@ -41,8 +40,14 @@
     return lax.axis_index("patch_3")
 
 
-def pack_kernel(fields, level, send, own, swap, rows, deep, cells, sems):
+def pack_kernel(fields, level_in, send_in, own, swap, rows, deep, cells, level, send, sems, small):
+    extras = [
+        pltpu.make_async_copy(level_in, level, small.at[0]),
+        pltpu.make_async_copy(send_in, send, small.at[1]),
+    ]
     copies = start_chunks(fields, cells, sems)
+    for extra in extras:
+        extra.start()
     width = 32 // CHUNKS
     fastest = jnp.zeros((32, 128), F32)
     for chunk in range(CHUNKS):
@@ -54,6 +59,8 @@
             return jnp.maximum(best, v + jnp.sqrt(h))
 
         fastest = lax.fori_loop(chunk * width, (chunk + 1) * width, speeds, fastest, unroll=True)
+    for extra in extras:
+        extra.wait()
     top = jnp.max(fastest, axis=0, keepdims=True)
     ratio = spacing_of(level[...]) / top
     swap[9 * T] = jnp.broadcast_to(jnp.min(ratio, axis=1, keepdims=True), (8, 128))
@@ -114,11 +121,18 @@
             jax.ShapeDtypeStruct((PACK, 128), F32),
             jax.ShapeDtypeStruct((DEEP, 128), F32),
         ),
-        in_specs=[ANY, VMEM, VMEM],
+        in_specs=[pl.BlockSpec(memory_space=pltpu.HBM)] * 3,
         out_specs=(VMEM,) * 4,
-        scratch_shapes=[pltpu.VMEM((4, 1024, 128), F32), pltpu.SemaphoreType.DMA((CHUNKS,))],
+        scratch_shapes=[
+            pltpu.VMEM((4, 1024, 128), F32),
+            pltpu.VMEM((1, 128), jnp.int32),
+            pltpu.VMEM((8, 16), jnp.int32),
+            pltpu.SemaphoreType.DMA((CHUNKS,)),
+            pltpu.SemaphoreType.DMA((2,)),
+        ],
+        compiler_params=pltpu.CompilerParams(vmem_limit_bytes=8 << 20),
         name="pack",
-    )(fields, level, send)
+    )(*[pltpu.with_memory_space_constraint(a, pltpu.HBM) for a in (fields, level, send)])
 
 
 def physical(q, normal):
@@ -137,19 +151,14 @@
     return [0.5 * (lf[c] + rf[c]) - widest * (right[c] - left[c]) for c in range(4)]
 
 
-def inner_kernel(fields, out, cells, lines, fluxes, sems):
-    copies = start_chunks(fields, cells, sems)
-    width = 32 // CHUNKS
-
+def inner_kernel(cells, out, lines, fluxes):
     def lay(x, carry):
         for c in range(4):
             line = cells[c, pl.ds(pl.multiple_of(32 * x, 32), 32), :]
             lines[pl.ds(c * SPAN + x * LINE + 2, 32), :] = line
         return carry
 
-    for chunk in range(CHUNKS):
-        copies[chunk].wait()
-        lax.fori_loop(chunk * width, (chunk + 1) * width, lay, 0, unroll=True)
+    lax.fori_loop(0, 32, lay, 0, unroll=4)
 
     def along_y(n, carry):
         r = 1 + 8 * n
@@ -210,24 +219,18 @@
     return pl.pallas_call(
         inner_kernel,
         out_shape=jax.ShapeDtypeStruct((4, 1024, 128), F32),
-        in_specs=[ANY],
+        in_specs=[VMEM],
         out_specs=VMEM,
-        scratch_shapes=[
-            pltpu.VMEM((4, 1024, 128), F32),
-            pltpu.VMEM((4 * SPAN, 128), F32),
-            pltpu.VMEM((4 * SPAN, 128), F32),
-            pltpu.SemaphoreType.DMA((CHUNKS,)),
-        ],
+        scratch_shapes=[pltpu.VMEM((4 * SPAN, 128), F32), pltpu.VMEM((4 * SPAN, 128), F32)],
+        compiler_params=pltpu.CompilerParams(vmem_limit_bytes=14 << 20),
         name="inner",
     )(fields)
 
 
 def step_kernel(
-    fields, inside, rows, deep, r1, r2, r3, r4, w, q, got, level, relation, half, refs,
-    out, step, cells, change, fresh, ghosts, pool, edge, weave, in_sems, change_sems, out_sems,
+    cells, inside, rows, deep, r1, r2, r3, r4, w, q, got, level, relation, half, refs,
+    out, step, fresh, ghosts, pool, edge, weave, out_sems,
 ):
-    field_copies = start_chunks(fields, cells, in_sems)
-    change_copies = start_chunks(inside, change, change_sems)
     sources = [
         (r1, T), (r1, 0), (r2, T), (r2, 0), (r3, T), (r3, 0), (r4, T), (r4, 0),
         (w, 8 * T), (q, T), (q, 0), (q, 3 * T), (q, 2 * T), (q, 5 * T), (q, 4 * T), (q, 6 * T),
@@ -291,65 +294,62 @@
                     ),
                 )
 
-    for copy in field_copies + change_copies:
-        copy.wait()
-
-    for face in range(4):
-
-        def border(j, carry):
-            def part(c, depth):
-                along = pl.multiple_of(8 * j, 8)
-                if depth < 0:
-                    return ghosts[pl.ds(((face * 4 + c) * 2 - depth - 1) * 32 + along, 8), :]
-                if face < 2:
-                    x = depth if face == 0 else 31 - depth
-                    return cells[c, pl.ds(32 * x + along, 8), :]
-                if depth < 2:
-                    return rows[pl.ds((face * 4 + c) * ROWS + 32 * depth + along, 8), :]
-                return deep[pl.ds(((face - 2) * 4 + c) * 64 + 32 * (depth - 2) + along, 8), :]
-
-            depths = [-2, -1, 0, 1, 2, 3]
-            if face % 2 == 1:
-                depths = depths[::-1]
-            q6 = [[part(c, depth) for c in range(4)] for depth in depths]
-            lean = [[0.25 * (q6[i + 1][c] - q6[i - 1][c]) for c in range(4)] for i in range(1, 5)]
-            flux = []
-            for i in range(1, 4):
-                left = [q6[i][c] + lean[i - 1][c] for c in range(4)]
-                right = [q6[i + 1][c] - lean[i][c] for c in range(4)]
-                flux.append(interface(left, right, 1 + face // 2))
-            for i in range(2):
-                depth = depths[i + 2]
-                where = depth if face % 2 == 0 else 31 - depth
-                for c in range(4):
-                    extra = flux[i + 1][c] - flux[i][c]
-                    if face < 2:
-                        spot = pl.ds(pl.multiple_of(32 * where + 8 * j, 8), 8)
-                    else:
-                        spot = pl.ds(256 * j + where, 8, stride=32)
-                    change[c, spot, :] = change[c, spot, :] + extra
-            return carry
-
-        lax.fori_loop(0, 4, border, 0, unroll=2)
-
     low = jnp.min(jnp.min(got[...], axis=0, keepdims=True), axis=1, keepdims=True)
     chosen = COURANT * low
     step[...] = chosen
     ratio = chosen / spacing_of(level[...])
 
-    out_copies = start_chunks(fresh, out, out_sems, inward=False)
-    width = 1024 // CHUNKS
-    for chunk in range(CHUNKS):
+    def border(face, j):
+        def part(c, depth):
+            if depth < 0:
+                return ghosts[pl.ds(((face * 4 + c) * 2 - depth - 1) * 32 + 8 * j, 8), :]
+            if face < 2:
+                x = depth if face == 0 else 31 - depth
+                return cells[c, pl.ds(32 * x + 8 * j, 8), :]
+            if depth < 2:
+                return rows[pl.ds((face * 4 + c) * ROWS + 32 * depth + 8 * j, 8), :]
+            return deep[pl.ds(((face - 2) * 4 + c) * 64 + 32 * (depth - 2) + 8 * j, 8), :]
+
+        depths = [-2, -1, 0, 1, 2, 3]
+        if face % 2 == 1:
+            depths = depths[::-1]
+        q6 = [[part(c, depth) for c in range(4)] for depth in depths]
+        lean = [[0.25 * (q6[i + 1][c] - q6[i - 1][c]) for c in range(4)] for i in range(1, 5)]
+        flux = []
+        for i in range(1, 4):
+            left = [q6[i][c] + lean[i - 1][c] for c in range(4)]
+            right = [q6[i + 1][c] - lean[i][c] for c in range(4)]
+            flux.append(interface(left, right, 1 + face // 2))
+        for i in range(2):
+            depth = depths[i + 2]
+            where = depth if face % 2 == 0 else 31 - depth
+            for c in range(4):
+                extra = flux[i + 1][c] - flux[i][c]
+                if face < 2:
+                    spot = pl.ds(32 * where + 8 * j, 8)
+                else:
+                    spot = pl.ds(256 * j + where, 8, stride=32)
+                fresh[c, spot, :] = fresh[c, spot, :] - ratio * extra
+
+    copies = []
+    for j in range(4):
 
         def update(n, carry):
-            spot = pl.ds(pl.multiple_of(chunk * width + 32 * n, 32), 32)
+            spot = pl.ds(pl.multiple_of(256 * j + 32 * n, 32), 32)
             for c in range(4):
-                fresh[c, spot, :] = cells[c, spot, :] - ratio * change[c, spot, :]
+                fresh[c, spot, :] = cells[c, spot, :] - ratio * inside[c, spot, :]
             return carry
 
-        lax.fori_loop(0, width // 32, update, 0, unroll=True)
-        out_copies[chunk].start()
-    for copy in out_copies:
+        lax.fori_loop(0, 8, update, 0, unroll=True)
+        for face in (2, 3):
+            border(face, j)
+        if j == 0 or j == 3:
+            for piece in range(4):
+                border(j // 3, piece)
+        part = pl.ds(256 * j, 256)
+        copies.append(pltpu.make_async_copy(fresh.at[:, part], out.at[:, part], out_sems.at[j]))
+        copies[-1].start()
+    for copy in copies:
         copy.wait()
 
 
@@ -360,20 +360,17 @@
             jax.ShapeDtypeStruct((4, 1024, 128), F32),
             jax.ShapeDtypeStruct((1, 1), F32),
         ),
-        in_specs=[ANY] * 2 + [VMEM] * 13,
+        in_specs=[VMEM] * 15,
         out_specs=(ANY, VMEM),
         scratch_shapes=[
-            pltpu.VMEM((4, 1024, 128), F32),
-            pltpu.VMEM((4, 1024, 128), F32),
             pltpu.VMEM((4, 1024, 128), F32),
             pltpu.VMEM((16 * 2 * 32, 128), F32),
             pltpu.VMEM((PACK, 128), F32),
             pltpu.VMEM((16 * 40, 128), F32),
             pltpu.VMEM((16 * 32, 128), F32),
-            pltpu.SemaphoreType.DMA((CHUNKS,)),
-            pltpu.SemaphoreType.DMA((CHUNKS,)),
-            pltpu.SemaphoreType.DMA((CHUNKS,)),
+            pltpu.SemaphoreType.DMA((4,)),
         ],
+        compiler_params=pltpu.CompilerParams(vmem_limit_bytes=18 << 20),
         name="advance",
     )(*operands)
 

time: 81.9 us -> 83.6 us (1.021)
  local copies, waits for them, and re-layouts: 3.21 us -> 11.2 us
  Pallas kernels: 17.2 us -> 10.4 us
  waiting for transfers between devices: 11.7 us -> 13.1 us
    unnamed x20 -> x28, local copies, waits for them, and re-layouts: 2.59 us -> 9.96 us
    pallas_call x1, Pallas kernels: 6.33 us -> 3.57 us  [inner(): pl.pallas_call(inner_kernel, out_shape=jax.ShapeDtypeStruct((4, 1024, 128...]
    pallas_call x1, Pallas kernels: 6.74 us -> 4.26 us  [advance(): pl.pallas_call(step_kernel, out_shape=(jax.ShapeDtypeStruct((4, 1024, 128...]
    pallas_call x1, Pallas kernels: 4.1 us -> 2.55 us  [pack(): pl.pallas_call(pack_kernel, out_shape=(tiles(7 * T), tiles(9 * T + 1), ja...]
    all_to_all x1, waiting for transfers between devices: 0.34 us -> 1.8 us  [compute(): lax.all_to_all(least, AXES, 0, 0, tiled=True, axis_index_groups=groups)]
  transfers between devices with their start and end apart: 7 -> 7, of which waited for: 4 -> 4; matrix products, arithmetic and copies ran while one was open for 2% -> 2% of each run, Pallas kernels for 8% -> 4%
where the time goes in v3:
time: 83.6 us; the launch traced here: 83.2 us
  starting transfers between devices  47.7 us (57%)
  waiting for transfers between devices  13.1 us (16%)
  local copies, waits for them, and re-layouts  11.2 us (13%)
  Pallas kernels  10.4 us (12%)
    ppermute x4, starting transfers between devices, two_way(): return lax.ppermute(array, AXES, pairs)  27.8 us
    ppermute x4, waiting for transfers between devices, two_way(): return lax.ppermute(array, AXES, pairs)  10 us
    unnamed x28, local copies, waits for them, and re-layouts  9.96 us
    ppermute x1, starting transfers between devices, swap_cores(): lax.ppermute(array, AXES, [(i, i ^ 1) for i in range(lax.axis_size(AXES))])  8.73 us
    all_to_all x1, starting transfers between devices, compute(): lax.all_to_all(least, AXES, 0, 0, tiled=True, axis_index_groups=groups)  7.56 us
    pallas_call x1, Pallas kernels, advance(): pl.pallas_call(step_kernel, out_shape=(jax.ShapeDtypeStruct((4, 1024, 128...  4.26 us
    pallas_call x1, Pallas kernels, inner(): pl.pallas_call(inner_kernel, out_shape=jax.ShapeDtypeStruct((4, 1024, 128...  3.57 us
    ppermute x1, starting transfers between devices, cross(): lax.ppermute(array, AXES, [(i, (i + (-3 if i % 2 else 3)) % n) for i in r...  3.56 us
  transfers between devices with their start and end apart: 7, of which 4 were waited for; matrix products, arithmetic and copies ran while one was open for 2% of the time, Pallas kernels for 4%

profile of v3, /device:TPU:1, one launch (start us, length us, event | category | flops | bytes accessed | tf_op | source)
XLA Modules:
  0.0 83.2 jit_solution(5728509780009835997)
XLA Ops:
  0.6 0.0 copy-start
  0.6 2.5 %pack.1 = (f32[70,8,128]{2,1,0:T(8,128)S(1)}, f32[91,8,128]{2,1,0:T(8,128)S(1)}, f32[1280,128]{1,0:T(8,128)S(1)}, f32[512,128]{1,0:T(8,128)S(1)}) custom-call(f32[4,1024,128]{2,1,0:T(8,128)} %bitcast.15, s32[1,128]{1,0:T(1,128)} %bitcast.21, s32[8,16]{1,0:T(8,128)} %bitcast.23), custom_call_target="tpu_custom_call" | custom-call | tf_op jit(solution)/shard_map/pack/pallas_call | solution.py:116
  3.2 0.0 copy-start.3
  3.2 0.7 copy-done.3
  3.9 8.7 %collective-permute-start = (f32[91,8,128]{2,1,0:T(8,128)S(1)}, f32[91,8,128]{2,1,0:T(8,128)S(1)}, u32[]{:S(2)}, u32[]{:S(2)}) collective-permute-start(f32[91,8,128]{2,1,0:T(8,128)S(1)} %get-tuple-element.11), channel_id=1, source_target_pairs={{0,1},{1,0},{2,3},{3,2},{4,5},{5,4},{6,7},{7,6},{8,9},{9,8},{10,11... | collective-permute-start | bytes 1118216 | tf_op jit(solution)/shard_map/ppermute | solution.py:385
  12.7 1.3 %collective-permute-done.w = f32[91,8,128]{2,1,0:T(8,128)S(1)} collective-permute-done((f32[91,8,128]{2,1,0:T(8,128)S(1)}, f32[91,8,128]{2,1,0:T(8,128)S(1)}, u32[]{:S(2)}, u32[]{:S(2)}) %collective-permute-start) | collective-permute-done | bytes 372768 | tf_op jit(solution)/shard_map/ppermute | solution.py:385
  14.0 0.6 slice_dynamic-update-slice_fusion.8
  14.6 0.6 slice_dynamic-update-slice_fusion.3
  15.2 11.7 %collective-permute-start.1 = (f32[21,8,128]{2,1,0:T(8,128)S(1)}, f32[21,8,128]{2,1,0:T(8,128)S(1)}, u32[]{:S(2)}, u32[]{:S(2)}) collective-permute-start(f32[21,8,128]{2,1,0:T(8,128)S(1)} %pad_maximum_fusion.1), channel_id=1, source_target_pairs={{0,8},{1,505},{2,10},{3,507},{4,12},{5,509},{6,14},{7,511},{8,16},... | collective-permute-start | bytes 258056 | tf_op jit(solution)/shard_map/ppermute | solution.py:381
  27.0 4.2 %collective-permute-done.1.r4 = f32[21,8,128]{2,1,0:T(8,128)S(1)} collective-permute-done((f32[21,8,128]{2,1,0:T(8,128)S(1)}, f32[21,8,128]{2,1,0:T(8,128)S(1)}, u32[]{:S(2)}, u32[]{:S(2)}) %collective-permute-start.1) | collective-permute-done | bytes 86048 | tf_op jit(solution)/shard_map/ppermute | solution.py:381
  31.1 8.1 %collective-permute-start.2 = (f32[41,8,128]{2,1,0:T(8,128)S(1)}, f32[41,8,128]{2,1,0:T(8,128)S(1)}, u32[]{:S(2)}, u32[]{:S(2)}) collective-permute-start(f32[41,8,128]{2,1,0:T(8,128)S(1)} %constant_dynamic-update-slice_fusion), channel_id=1, source_target_pairs={{0,2},{1,511},{2,4},{3,1},{4,6},{5,3},{6,8},{7,5},{8,10},{9,7},{10... | collective-permute-start | bytes 503816 | tf_op jit(solution)/shard_map/ppermute | solution.py:381
  39.3 6.0 %collective-permute-start.4 = (f32[31,8,128]{2,1,0:T(8,128)S(1)}, f32[31,8,128]{2,1,0:T(8,128)S(1)}, u32[]{:S(2)}, u32[]{:S(2)}) collective-permute-start(f32[31,8,128]{2,1,0:T(8,128)S(1)} %pad_maximum_fusion), channel_id=1, source_target_pairs={{0,6},{1,507},{2,8},{3,509},{4,10},{5,511},{6,12},{7,1},{8,14},{9,... | collective-permute-start | bytes 380936 | tf_op jit(solution)/shard_map/ppermute | solution.py:381
  45.3 1.9 %collective-permute-start.3 = (f32[41,8,128]{2,1,0:T(8,128)S(1)}, f32[41,8,128]{2,1,0:T(8,128)S(1)}, u32[]{:S(2)}, u32[]{:S(2)}) collective-permute-start(f32[41,8,128]{2,1,0:T(8,128)S(1)} %get-tuple-element.14), channel_id=1, source_target_pairs={{0,4},{1,509},{2,6},{3,511},{4,8},{5,1},{6,10},{7,3},{8,12},{9,5},... | collective-permute-start | bytes 503816 | tf_op jit(solution)/shard_map/ppermute | solution.py:381
  47.2 0.0 collective-permute-done.2.r1
  47.2 0.6 slice_dynamic-update-slice_fusion.1
  47.9 5.8 %collective-permute-done.3.r2 = f32[41,8,128]{2,1,0:T(8,128)S(1)} collective-permute-done((f32[41,8,128]{2,1,0:T(8,128)S(1)}, f32[41,8,128]{2,1,0:T(8,128)S(1)}, u32[]{:S(2)}, u32[]{:S(2)}) %collective-permute-start.3) | collective-permute-done | bytes 167968 | tf_op jit(solution)/shard_map/ppermute | solution.py:381
  53.7 0.6 slice_dynamic-update-slice_fusion
  54.4 0.0 collective-permute-done.4.r3
  54.4 0.6 slice_dynamic-update-slice_fusion.2
  55.0 3.6 %collective-permute-start.5 = (f32[70,8,128]{2,1,0:T(8,128)}, f32[70,8,128]{2,1,0:T(8,128)}, u32[]{:S(2)}, u32[]{:S(2)}) collective-permute-start(f32[70,8,128]{2,1,0:T(8,128)} %slice_dynamic-update-slice_fusion.2), channel_id=1, source_target_pairs={{0,3},{1,510},{2,5},{3,0},{4,7},{5,2},{6,9},{7,4},{8,11},{9,6},{10... | collective-permute-start | bytes 860168 | tf_op jit(solution)/shard_map/ppermute | solution.py:390
  58.6 0.0 copy-start.5
  58.6 0.6 copy-done.5
  59.2 0.6 broadcast_in_dim.2
  59.8 7.6 %all-to-all-start = ((f32[32,1,128]{2,1,0:T(1,128)}), f32[32,1,128]{2,1,0:T(1,128)}, u32[]{:S(2)}, u32[]{:S(2)}) async-start(f32[32,1,128]{2,1,0:T(1,128)} %broadcast_in_dim.2), calls=%async_computation | async-start | bytes 32768 | tf_op jit(solution)/shard_map/all_to_all | solution.py:426
  67.4 0.0 copy-done
  67.4 0.0 copy-start.7
  67.4 0.0 copy-start.8
  67.4 3.6 %inner.1.inside = f32[4,1024,128]{2,1,0:T(8,128)S(1)} custom-call(f32[4,1024,128]{2,1,0:T(8,128)S(1)} %bitcast.16), custom_call_target="tpu_custom_call" | custom-call | tf_op jit(solution)/shard_map/inner/pallas_call | solution.py:219
  71.0 0.0 copy-start.1
  71.0 1.3 %copy-done.1 = f32[4,1024,128]{2,1,0:T(8,128)} copy-done((f32[4,1024,128]{2,1,0:T(8,128)}, f32[4,1024,128]{2,1,0:T(8,128)S(1)}, u32[]{:S(2)}) %copy-start.1) | copy-done | bytes 2097176
  72.3 1.8 %all-to-all-done = f32[32,1,128]{2,1,0:T(1,128)} async-done(((f32[32,1,128]{2,1,0:T(1,128)}), f32[32,1,128]{2,1,0:T(1,128)}, u32[]{:S(2)}, u32[]{:S(2)}) %all-to-all-start) | async-done | bytes 16416 | tf_op jit(solution)/shard_map/all_to_all | solution.py:426
  74.1 0.0 collective-permute-done.5.q
  74.1 0.0 copy-done.7
  74.1 0.0 copy-done.8
  74.1 0.0 copy-start.2
  74.1 1.6 %copy-done.2 = f32[4,1024,128]{2,1,0:T(8,128)S(1)} copy-done((f32[4,1024,128]{2,1,0:T(8,128)S(1)}, f32[4,1024,128]{2,1,0:T(8,128)}, u32[]{:S(2)}) %copy-start.2) | copy-done | bytes 2097176
  75.7 0.0 copy-start.4
  75.7 0.9 %copy-done.4 = f32[512,128]{1,0:T(8,128)S(1)} copy-done((f32[512,128]{1,0:T(8,128)S(1)}, f32[512,128]{1,0:T(8,128)}, u32[]{:S(2)}) %copy-start.4) | copy-done | bytes 262168
  76.7 0.0 copy-start.6
  76.7 0.9 %copy-done.6 = f32[31,8,128]{2,1,0:T(8,128)S(1)} copy-done((f32[31,8,128]{2,1,0:T(8,128)S(1)}, f32[31,8,128]{2,1,0:T(8,128)}, u32[]{:S(2)}) %copy-start.6) | copy-done | bytes 127000
  77.6 0.0 copy-start.9
  77.6 0.7 copy-done.9
  78.3 0.0 copy-start.10
  78.3 0.7 copy-done.10
  78.9 4.3 %advance.1 = (f32[4,1024,128]{2,1,0:T(8,128)}, f32[1,1]{1,0:T(1,128)}) custom-call(f32[4,1024,128]{2,1,0:T(8,128)S(1)} %bitcast.17, f32[4,1024,128]{2,1,0:T(8,128)S(1)} %copy-done.2, f32[1280,128]{1,0:T(8,128)S(1)} %get-tuple-element.8.rows, f32[512,128]{1,0:T(8,128)S(1)} %copy-done.4, f32[41,8,128]{2,1,0:T(8,128)S(1)} %collective-permute-done.2.r1, ...), custom_call_target="tpu_custom_call" | custom-call | tf_op jit(solution)/shard_map/advance/pallas_call | solution.py:357
  (9 shorter events, 0.1 us)
Async XLA Ops:
  0.6 66.8 %copy-start = (f32[4,32,32,128]{3,2,1,0:T(8,128)S(1)}, f32[4,32,32,128]{3,2,1,0:T(8,128)}, u32[]{:S(2)}) copy-start(f32[4,32,32,128]{3,2,1,0:T(8,128)} %param.6) | copy-start | bytes 6291460
  3.2 0.7 copy-start.3
  3.9 10.0 %collective-permute-start = (f32[91,8,128]{2,1,0:T(8,128)S(1)}, f32[91,8,128]{2,1,0:T(8,128)S(1)}, u32[]{:S(2)}, u32[]{:S(2)}) collective-permute-start(f32[91,8,128]{2,1,0:T(8,128)S(1)} %get-tuple-element.11), channel_id=1, source_target_pairs={{0,1},{1,0},{2,3},{3,2},{4,5},{5,4},{6,7},{7,6},{8,9},{9,8},{10,11... | collective-permute-start | bytes 1118216 | tf_op jit(solution)/shard_map/ppermute | solution.py:385
  15.2 15.9 %collective-permute-start.1 = (f32[21,8,128]{2,1,0:T(8,128)S(1)}, f32[21,8,128]{2,1,0:T(8,128)S(1)}, u32[]{:S(2)}, u32[]{:S(2)}) collective-permute-start(f32[21,8,128]{2,1,0:T(8,128)S(1)} %pad_maximum_fusion.1), channel_id=1, source_target_pairs={{0,8},{1,505},{2,10},{3,507},{4,12},{5,509},{6,14},{7,511},{8,16},... | collective-permute-start | bytes 258056 | tf_op jit(solution)/shard_map/ppermute | solution.py:381
  31.1 16.1 %collective-permute-start.2 = (f32[41,8,128]{2,1,0:T(8,128)S(1)}, f32[41,8,128]{2,1,0:T(8,128)S(1)}, u32[]{:S(2)}, u32[]{:S(2)}) collective-permute-start(f32[41,8,128]{2,1,0:T(8,128)S(1)} %constant_dynamic-update-slice_fusion), channel_id=1, source_target_pairs={{0,2},{1,511},{2,4},{3,1},{4,6},{5,3},{6,8},{7,5},{8,10},{9,7},{10... | collective-permute-start | bytes 503816 | tf_op jit(solution)/shard_map/ppermute | solution.py:381
  39.3 15.1 %collective-permute-start.4 = (f32[31,8,128]{2,1,0:T(8,128)S(1)}, f32[31,8,128]{2,1,0:T(8,128)S(1)}, u32[]{:S(2)}, u32[]{:S(2)}) collective-permute-start(f32[31,8,128]{2,1,0:T(8,128)S(1)} %pad_maximum_fusion), channel_id=1, source_target_pairs={{0,6},{1,507},{2,8},{3,509},{4,10},{5,511},{6,12},{7,1},{8,14},{9,... | collective-permute-start | bytes 380936 | tf_op jit(solution)/shard_map/ppermute | solution.py:381
  45.3 8.4 %collective-permute-start.3 = (f32[41,8,128]{2,1,0:T(8,128)S(1)}, f32[41,8,128]{2,1,0:T(8,128)S(1)}, u32[]{:S(2)}, u32[]{:S(2)}) collective-permute-start(f32[41,8,128]{2,1,0:T(8,128)S(1)} %get-tuple-element.14), channel_id=1, source_target_pairs={{0,4},{1,509},{2,6},{3,511},{4,8},{5,1},{6,10},{7,3},{8,12},{9,5},... | collective-permute-start | bytes 503816 | tf_op jit(solution)/shard_map/ppermute | solution.py:381
  55.0 19.1 %collective-permute-start.5 = (f32[70,8,128]{2,1,0:T(8,128)}, f32[70,8,128]{2,1,0:T(8,128)}, u32[]{:S(2)}, u32[]{:S(2)}) collective-permute-start(f32[70,8,128]{2,1,0:T(8,128)} %slice_dynamic-update-slice_fusion.2), channel_id=1, source_target_pairs={{0,3},{1,510},{2,5},{3,0},{4,7},{5,2},{6,9},{7,4},{8,11},{9,6},{10... | collective-permute-start | bytes 860168 | tf_op jit(solution)/shard_map/ppermute | solution.py:390
  58.6 0.6 copy-start.5
  59.8 14.3 %all-to-all-start = ((f32[32,1,128]{2,1,0:T(1,128)}), f32[32,1,128]{2,1,0:T(1,128)}, u32[]{:S(2)}, u32[]{:S(2)}) async-start(f32[32,1,128]{2,1,0:T(1,128)} %broadcast_in_dim.2), calls=%async_computation | async-start | bytes 32768 | tf_op jit(solution)/shard_map/all_to_all | solution.py:426
  67.4 6.7 %copy-start.7 = (s32[128,4,2]{0,2,1:T(2,128)S(1)}, s32[128,4,2]{0,2,1:T(2,128)}, u32[]{:S(2)}) copy-start(s32[128,4,2]{0,2,1:T(2,128)} %param.10) | copy-start | bytes 12292
  67.4 6.7 %copy-start.8 = (s32[128,4]{0,1:T(4,128)S(1)}, s32[128,4]{0,1:T(4,128)}, u32[]{:S(2)}) copy-start(s32[128,4]{0,1:T(4,128)} %param.8) | copy-start | bytes 6148
  71.0 1.3 %copy-start.1 = (f32[4,1024,128]{2,1,0:T(8,128)}, f32[4,1024,128]{2,1,0:T(8,128)S(1)}, u32[]{:S(2)}) copy-start(f32[4,1024,128]{2,1,0:T(8,128)S(1)} %inner.1.inside) | copy-start | bytes 6291460
  74.1 1.6 %copy-start.2 = (f32[4,1024,128]{2,1,0:T(8,128)S(1)}, f32[4,1024,128]{2,1,0:T(8,128)}, u32[]{:S(2)}) copy-start(f32[4,1024,128]{2,1,0:T(8,128)} %copy-done.1) | copy-start | bytes 6291460
  75.7 0.9 %copy-start.4 = (f32[512,128]{1,0:T(8,128)S(1)}, f32[512,128]{1,0:T(8,128)}, u32[]{:S(2)}) copy-start(f32[512,128]{1,0:T(8,128)} %copy-done.3) | copy-start | bytes 786436
  76.7 0.9 %copy-start.6 = (f32[31,8,128]{2,1,0:T(8,128)S(1)}, f32[31,8,128]{2,1,0:T(8,128)}, u32[]{:S(2)}) copy-start(f32[31,8,128]{2,1,0:T(8,128)} %copy-done.5) | copy-start | bytes 380932
  77.6 0.7 copy-start.9
  78.3 0.7 copy-start.10

commit v4 on v3

--- a/solution.py
+++ b/solution.py
@@ -406,23 +406,25 @@
         return blk(w, j - 1)
 
     low = jnp.minimum(swap[9 * T :], w[9 * T :])
-    r4 = two_way(jnp.concatenate([ahead(8), beside(7), low]), 4)
-    inside = inner(flat)
-    low = jnp.minimum(low, r4[2 * T :])
     r3 = two_way(jnp.concatenate([ahead(6), beside(5), beside(8), low]), 3)
     r2 = two_way(jnp.concatenate([ahead(4), beside(3), ahead(7), beside(6), low]), 2)
     r1 = two_way(jnp.concatenate([ahead(2), beside(1), ahead(5), beside(4), low]), 1)
+    r4 = two_way(jnp.concatenate([ahead(8), beside(7)]), 4)
+    low = jnp.minimum(jnp.minimum(low, r1[4 * T :]), jnp.minimum(r2[4 * T :], r3[3 * T :]))
+    beyond = two_way(low, 4)
     q = cross(
         jnp.concatenate([ahead(3), beside(2), blk(r1, 2, 2), blk(r2, 2, 2), blk(r3, 2)])
     )
+    inside = inner(flat)
     depth = lax.axis_size("patch_2")
     columns = lax.axis_size(("patch_0", "patch_1"))
-    low = jnp.minimum(jnp.minimum(low, r1[4 * T :]), jnp.minimum(r2[4 * T :], r3[3 * T :]))
+    low = jnp.minimum(low, beyond)
     least = jnp.broadcast_to(low[0, :1], (2 * columns, 128))
     groups = [
         [(r * depth + (g + c) % depth) * 2 + c for r in range(columns) for c in range(2)]
         for g in range(depth)
     ]
+    least, r4 = lax.optimization_barrier((least, r4))
     got = lax.all_to_all(least, AXES, 0, 0, tiled=True, axis_index_groups=groups)
     advanced, step = advance(
         flat, inside, rows, deep, r1, r2, r3, r4, w, q, got, level, relation.T, face_half.T,

time: 83.6 us -> 72.8 us (0.87)
  the two profiles are of different devices: /device:TPU:1 before, /device:TPU:32 now
where the time goes in v4:
time: 72.8 us; the launch traced here: 72.4 us
  starting transfers between devices  42 us (58%)
  Pallas kernels  10.4 us (14%)
  local copies, waits for them, and re-layouts  9.9 us (14%)
  waiting for transfers between devices  9.2 us (13%)
  between operations  0.86 us (1%)
    ppermute x5, starting transfers between devices, two_way(): return lax.ppermute(array, AXES, pairs)  25.1 us
    ppermute x1, starting transfers between devices, cross(): lax.ppermute(array, AXES, [(i, (i + (-3 if i % 2 else 3)) % n) for i in r...  10.6 us
    unnamed x28, local copies, waits for them, and re-layouts  8.68 us
    ppermute x5, waiting for transfers between devices, two_way(): return lax.ppermute(array, AXES, pairs)  4.98 us
    all_to_all x1, starting transfers between devices, compute(): lax.all_to_all(least, AXES, 0, 0, tiled=True, axis_index_groups=groups)  4.49 us
    pallas_call x1, Pallas kernels, advance(): pl.pallas_call(step_kernel, out_shape=(jax.ShapeDtypeStruct((4, 1024, 128...  4.25 us
    pallas_call x1, Pallas kernels, inner(): pl.pallas_call(inner_kernel, out_shape=jax.ShapeDtypeStruct((4, 1024, 128...  3.57 us
    all_to_all x1, waiting for transfers between devices, compute(): lax.all_to_all(least, AXES, 0, 0, tiled=True, axis_index_groups=groups)  2.57 us
  transfers between devices with their start and end apart: 8, of which 3 were waited for; matrix products, arithmetic and copies ran while one was open for 4% of the time, Pallas kernels for 5%

profile of v4, /device:TPU:32, one launch (start us, length us, event | category | flops | bytes accessed | tf_op | source)
XLA Modules:
  0.0 72.4 jit_solution(12524905108188865267)
XLA Ops:
  0.6 0.0 copy-start
  0.6 2.5 %pack.1 = (f32[70,8,128]{2,1,0:T(8,128)S(1)}, f32[91,8,128]{2,1,0:T(8,128)S(1)}, f32[1280,128]{1,0:T(8,128)S(1)}, f32[512,128]{1,0:T(8,128)S(1)}) custom-call(f32[4,1024,128]{2,1,0:T(8,128)} %bitcast.16, s32[1,128]{1,0:T(1,128)} %bitcast.22, s32[8,16]{1,0:T(8,128)} %bitcast.25), custom_call_target="tpu_custom_call" | custom-call | tf_op jit(solution)/shard_map/pack/pallas_call | solution.py:116
  3.2 0.0 copy-start.3
  3.2 0.7 copy-done.3
  3.9 1.9 %collective-permute-start = (f32[91,8,128]{2,1,0:T(8,128)S(1)}, f32[91,8,128]{2,1,0:T(8,128)S(1)}, u32[]{:S(2)}, u32[]{:S(2)}) collective-permute-start(f32[91,8,128]{2,1,0:T(8,128)S(1)} %get-tuple-element.13), channel_id=1, source_target_pairs={{0,1},{1,0},{2,3},{3,2},{4,5},{5,4},{6,7},{7,6},{8,9},{9,8},{10,11... | collective-permute-start | bytes 1118216 | tf_op jit(solution)/shard_map/ppermute | solution.py:385
  5.8 1.6 %collective-permute-done.w = f32[91,8,128]{2,1,0:T(8,128)S(1)} collective-permute-done((f32[91,8,128]{2,1,0:T(8,128)S(1)}, f32[91,8,128]{2,1,0:T(8,128)S(1)}, u32[]{:S(2)}, u32[]{:S(2)}) %collective-permute-start) | collective-permute-done | bytes 372768 | tf_op jit(solution)/shard_map/ppermute | solution.py:385
  7.5 0.6 slice_dynamic-update-slice_fusion.8
  8.1 0.6 slice_dynamic-update-slice_fusion.3
  8.8 3.8 %collective-permute-start.1 = (f32[41,8,128]{2,1,0:T(8,128)S(1)}, f32[41,8,128]{2,1,0:T(8,128)S(1)}, u32[]{:S(2)}, u32[]{:S(2)}) collective-permute-start(f32[41,8,128]{2,1,0:T(8,128)S(1)} %constant_dynamic-update-slice_fusion), channel_id=1, source_target_pairs={{0,2},{1,511},{2,4},{3,1},{4,6},{5,3},{6,8},{7,5},{8,10},{9,7},{10... | collective-permute-start | bytes 503816 | tf_op jit(solution)/shard_map/ppermute | solution.py:381
  12.6 6.4 %collective-permute-start.2 = (f32[41,8,128]{2,1,0:T(8,128)S(1)}, f32[41,8,128]{2,1,0:T(8,128)S(1)}, u32[]{:S(2)}, u32[]{:S(2)}) collective-permute-start(f32[41,8,128]{2,1,0:T(8,128)S(1)} %get-tuple-element.18), channel_id=1, source_target_pairs={{0,4},{1,509},{2,6},{3,511},{4,8},{5,1},{6,10},{7,3},{8,12},{9,5},... | collective-permute-start | bytes 503816 | tf_op jit(solution)/shard_map/ppermute | solution.py:381
  19.0 6.5 %collective-permute-start.3 = (f32[31,8,128]{2,1,0:T(8,128)S(1)}, f32[31,8,128]{2,1,0:T(8,128)S(1)}, u32[]{:S(2)}, u32[]{:S(2)}) collective-permute-start(f32[31,8,128]{2,1,0:T(8,128)S(1)} %pad_maximum_fusion), channel_id=1, source_target_pairs={{0,6},{1,507},{2,8},{3,509},{4,10},{5,511},{6,12},{7,1},{8,14},{9,... | collective-permute-start | bytes 380936 | tf_op jit(solution)/shard_map/ppermute | solution.py:381
  25.5 6.4 %collective-permute-start.5 = (f32[20,8,128]{2,1,0:T(8,128)S(1)}, f32[20,8,128]{2,1,0:T(8,128)S(1)}, u32[]{:S(2)}, u32[]{:S(2)}) collective-permute-start(f32[20,8,128]{2,1,0:T(8,128)S(1)} %pad_maximum_fusion.1), channel_id=1, source_target_pairs={{0,8},{1,505},{2,10},{3,507},{4,12},{5,509},{6,14},{7,511},{8,16},... | collective-permute-start | bytes 245768 | tf_op jit(solution)/shard_map/ppermute | solution.py:381
  32.0 5.0 %collective-permute-done.3.r3 = f32[31,8,128]{2,1,0:T(8,128)S(1)} collective-permute-done((f32[31,8,128]{2,1,0:T(8,128)S(1)}, f32[31,8,128]{2,1,0:T(8,128)S(1)}, u32[]{:S(2)}, u32[]{:S(2)}) %collective-permute-start.3) | collective-permute-done | bytes 127008 | tf_op jit(solution)/shard_map/ppermute | solution.py:381
  36.9 0.0 copy-start.5
  36.9 0.0 collective-permute-done.1.r1
  36.9 0.0 collective-permute-done.2.r2
  37.0 1.9 %collective-permute-start.4 = (f32[1,8,128]{2,1,0:T(8,128)S(1)}, f32[1,8,128]{2,1,0:T(8,128)S(1)}, u32[]{:S(2)}, u32[]{:S(2)}) collective-permute-start(f32[1,8,128]{2,1,0:T(8,128)S(1)} %fusion), channel_id=1, source_target_pairs={{0,8},{1,505},{2,10},{3,507},{4,12},{5,509},{6,14},{7,511},{8,16},... | collective-permute-start | bytes 12296 | tf_op jit(solution)/shard_map/ppermute | solution.py:381
  38.9 0.6 slice_dynamic-update-slice_fusion.1
  39.5 0.6 slice_dynamic-update-slice_fusion
  40.2 0.0 copy-done.5
  40.2 0.6 slice_dynamic-update-slice_fusion.2
  40.8 10.6 %collective-permute-start.6 = (f32[70,8,128]{2,1,0:T(8,128)}, f32[70,8,128]{2,1,0:T(8,128)}, u32[]{:S(2)}, u32[]{:S(2)}) collective-permute-start(f32[70,8,128]{2,1,0:T(8,128)} %slice_dynamic-update-slice_fusion.2), channel_id=1, source_target_pairs={{0,3},{1,510},{2,5},{3,0},{4,7},{5,2},{6,9},{7,4},{8,11},{9,6},{10... | collective-permute-start | bytes 860168 | tf_op jit(solution)/shard_map/ppermute | solution.py:390
  51.4 0.0 collective-permute-done.4
  51.4 0.0 collective-permute-done.5.r4
  51.4 0.6 broadcast_in_dim.8
  52.0 4.5 %all-to-all-start = ((f32[32,1,128]{2,1,0:T(1,128)}), f32[32,1,128]{2,1,0:T(1,128)}, u32[]{:S(2)}, u32[]{:S(2)}) async-start(f32[32,1,128]{2,1,0:T(1,128)} %bitcast.24), calls=%async_computation | async-start | bytes 32768 | tf_op jit(solution)/shard_map/all_to_all | solution.py:428
  56.5 0.0 copy-done
  56.5 0.0 copy-start.7
  56.5 0.0 copy-start.8
  56.5 0.0 copy-start.9
  56.5 3.6 %inner.1.inside = f32[4,1024,128]{2,1,0:T(8,128)S(1)} custom-call(f32[4,1024,128]{2,1,0:T(8,128)S(1)} %bitcast.17), custom_call_target="tpu_custom_call" | custom-call | tf_op jit(solution)/shard_map/inner/pallas_call | solution.py:219
  60.1 0.0 copy-start.1
  60.1 1.3 %copy-done.1 = f32[4,1024,128]{2,1,0:T(8,128)} copy-done((f32[4,1024,128]{2,1,0:T(8,128)}, f32[4,1024,128]{2,1,0:T(8,128)S(1)}, u32[]{:S(2)}) %copy-start.1) | copy-done | bytes 2097176
  61.4 2.6 %all-to-all-done = f32[32,1,128]{2,1,0:T(1,128)} async-done(((f32[32,1,128]{2,1,0:T(1,128)}), f32[32,1,128]{2,1,0:T(1,128)}, u32[]{:S(2)}, u32[]{:S(2)}) %all-to-all-start) | async-done | bytes 16416 | tf_op jit(solution)/shard_map/all_to_all | solution.py:428
  64.0 0.0 collective-permute-done.6.q
  64.0 0.0 copy-done.7
  64.0 0.0 copy-done.8
  64.0 0.0 copy-done.9
  64.0 0.0 copy-start.2
  64.0 1.6 %copy-done.2 = f32[4,1024,128]{2,1,0:T(8,128)S(1)} copy-done((f32[4,1024,128]{2,1,0:T(8,128)S(1)}, f32[4,1024,128]{2,1,0:T(8,128)}, u32[]{:S(2)}) %copy-start.2) | copy-done | bytes 2097176
  65.6 0.0 copy-start.4
  65.6 0.9 %copy-done.4 = f32[512,128]{1,0:T(8,128)S(1)} copy-done((f32[512,128]{1,0:T(8,128)S(1)}, f32[512,128]{1,0:T(8,128)}, u32[]{:S(2)}) %copy-start.4) | copy-done | bytes 262168
  66.6 0.0 copy-start.6
  66.6 0.9 %copy-done.6 = f32[31,8,128]{2,1,0:T(8,128)S(1)} copy-done((f32[31,8,128]{2,1,0:T(8,128)S(1)}, f32[31,8,128]{2,1,0:T(8,128)}, u32[]{:S(2)}) %copy-start.6) | copy-done | bytes 127000
  67.5 0.0 copy-start.10
  67.5 0.7 copy-done.10
  68.1 4.3 %advance.1 = (f32[4,1024,128]{2,1,0:T(8,128)}, f32[1,1]{1,0:T(1,128)}) custom-call(f32[4,1024,128]{2,1,0:T(8,128)S(1)} %bitcast.18, f32[4,1024,128]{2,1,0:T(8,128)S(1)} %copy-done.2, f32[1280,128]{1,0:T(8,128)S(1)} %get-tuple-element.10.rows, f32[512,128]{1,0:T(8,128)S(1)} %copy-done.4, f32[41,8,128]{2,1,0:T(8,128)S(1)} %collective-permute-done.1.r1, ...), custom_call_target="tpu_custom_call" | custom-call | tf_op jit(solution)/shard_map/advance/pallas_call | solution.py:357
  (9 shorter events, 0.1 us)
Async XLA Ops:
  0.6 55.9 %copy-start = (f32[4,32,32,128]{3,2,1,0:T(8,128)S(1)}, f32[4,32,32,128]{3,2,1,0:T(8,128)}, u32[]{:S(2)}) copy-start(f32[4,32,32,128]{3,2,1,0:T(8,128)} %param.6) | copy-start | bytes 6291460
  3.2 0.7 copy-start.3
  3.9 3.6 %collective-permute-start = (f32[91,8,128]{2,1,0:T(8,128)S(1)}, f32[91,8,128]{2,1,0:T(8,128)S(1)}, u32[]{:S(2)}, u32[]{:S(2)}) collective-permute-start(f32[91,8,128]{2,1,0:T(8,128)S(1)} %get-tuple-element.13), channel_id=1, source_target_pairs={{0,1},{1,0},{2,3},{3,2},{4,5},{5,4},{6,7},{7,6},{8,9},{9,8},{10,11... | collective-permute-start | bytes 1118216 | tf_op jit(solution)/shard_map/ppermute | solution.py:385
  8.8 28.2 %collective-permute-start.1 = (f32[41,8,128]{2,1,0:T(8,128)S(1)}, f32[41,8,128]{2,1,0:T(8,128)S(1)}, u32[]{:S(2)}, u32[]{:S(2)}) collective-permute-start(f32[41,8,128]{2,1,0:T(8,128)S(1)} %constant_dynamic-update-slice_fusion), channel_id=1, source_target_pairs={{0,2},{1,511},{2,4},{3,1},{4,6},{5,3},{6,8},{7,5},{8,10},{9,7},{10... | collective-permute-start | bytes 503816 | tf_op jit(solution)/shard_map/ppermute | solution.py:381
  12.6 24.4 %collective-permute-start.2 = (f32[41,8,128]{2,1,0:T(8,128)S(1)}, f32[41,8,128]{2,1,0:T(8,128)S(1)}, u32[]{:S(2)}, u32[]{:S(2)}) collective-permute-start(f32[41,8,128]{2,1,0:T(8,128)S(1)} %get-tuple-element.18), channel_id=1, source_target_pairs={{0,4},{1,509},{2,6},{3,511},{4,8},{5,1},{6,10},{7,3},{8,12},{9,5},... | collective-permute-start | bytes 503816 | tf_op jit(solution)/shard_map/ppermute | solution.py:381
  19.0 17.9 %collective-permute-start.3 = (f32[31,8,128]{2,1,0:T(8,128)S(1)}, f32[31,8,128]{2,1,0:T(8,128)S(1)}, u32[]{:S(2)}, u32[]{:S(2)}) collective-permute-start(f32[31,8,128]{2,1,0:T(8,128)S(1)} %pad_maximum_fusion), channel_id=1, source_target_pairs={{0,6},{1,507},{2,8},{3,509},{4,10},{5,511},{6,12},{7,1},{8,14},{9,... | collective-permute-start | bytes 380936 | tf_op jit(solution)/shard_map/ppermute | solution.py:381
  25.5 25.8 %collective-permute-start.5 = (f32[20,8,128]{2,1,0:T(8,128)S(1)}, f32[20,8,128]{2,1,0:T(8,128)S(1)}, u32[]{:S(2)}, u32[]{:S(2)}) collective-permute-start(f32[20,8,128]{2,1,0:T(8,128)S(1)} %pad_maximum_fusion.1), channel_id=1, source_target_pairs={{0,8},{1,505},{2,10},{3,507},{4,12},{5,509},{6,14},{7,511},{8,16},... | collective-permute-start | bytes 245768 | tf_op jit(solution)/shard_map/ppermute | solution.py:381
  36.9 3.2 %copy-start.5 = (f32[31,8,128]{2,1,0:T(8,128)}, f32[31,8,128]{2,1,0:T(8,128)S(1)}, u32[]{:S(2)}) copy-start(f32[31,8,128]{2,1,0:T(8,128)S(1)} %collective-permute-done.3.r3) | copy-start | bytes 380932
  37.0 14.4 %collective-permute-start.4 = (f32[1,8,128]{2,1,0:T(8,128)S(1)}, f32[1,8,128]{2,1,0:T(8,128)S(1)}, u32[]{:S(2)}, u32[]{:S(2)}) collective-permute-start(f32[1,8,128]{2,1,0:T(8,128)S(1)} %fusion), channel_id=1, source_target_pairs={{0,8},{1,505},{2,10},{3,507},{4,12},{5,509},{6,14},{7,511},{8,16},... | collective-permute-start | bytes 12296 | tf_op jit(solution)/shard_map/ppermute | solution.py:381
  40.8 23.2 %collective-permute-start.6 = (f32[70,8,128]{2,1,0:T(8,128)}, f32[70,8,128]{2,1,0:T(8,128)}, u32[]{:S(2)}, u32[]{:S(2)}) collective-permute-start(f32[70,8,128]{2,1,0:T(8,128)} %slice_dynamic-update-slice_fusion.2), channel_id=1, source_target_pairs={{0,3},{1,510},{2,5},{3,0},{4,7},{5,2},{6,9},{7,4},{8,11},{9,6},{10... | collective-permute-start | bytes 860168 | tf_op jit(solution)/shard_map/ppermute | solution.py:390
  52.0 12.0 %all-to-all-start = ((f32[32,1,128]{2,1,0:T(1,128)}), f32[32,1,128]{2,1,0:T(1,128)}, u32[]{:S(2)}, u32[]{:S(2)}) async-start(f32[32,1,128]{2,1,0:T(1,128)} %bitcast.24), calls=%async_computation | async-start | bytes 32768 | tf_op jit(solution)/shard_map/all_to_all | solution.py:428
  56.5 7.5 %copy-start.7 = (s32[128,4,2]{0,2,1:T(2,128)S(1)}, s32[128,4,2]{0,2,1:T(2,128)}, u32[]{:S(2)}) copy-start(s32[128,4,2]{0,2,1:T(2,128)} %param.10) | copy-start | bytes 12292
  56.5 7.5 %copy-start.8 = (s32[128,4]{0,1:T(4,128)S(1)}, s32[128,4]{0,1:T(4,128)}, u32[]{:S(2)}) copy-start(s32[128,4]{0,1:T(4,128)} %param.8) | copy-start | bytes 6148
  56.5 7.5 %copy-start.9 = (s32[128,4]{0,1:T(4,128)S(1)}, s32[128,4]{0,1:T(4,128)}, u32[]{:S(2)}) copy-start(s32[128,4]{0,1:T(4,128)} %param.9) | copy-start | bytes 6148
  60.1 1.3 %copy-start.1 = (f32[4,1024,128]{2,1,0:T(8,128)}, f32[4,1024,128]{2,1,0:T(8,128)S(1)}, u32[]{:S(2)}) copy-start(f32[4,1024,128]{2,1,0:T(8,128)S(1)} %inner.1.inside) | copy-start | bytes 6291460
  64.0 1.6 %copy-start.2 = (f32[4,1024,128]{2,1,0:T(8,128)S(1)}, f32[4,1024,128]{2,1,0:T(8,128)}, u32[]{:S(2)}) copy-start(f32[4,1024,128]{2,1,0:T(8,128)} %copy-done.1) | copy-start | bytes 6291460
  65.6 0.9 %copy-start.4 = (f32[512,128]{1,0:T(8,128)S(1)}, f32[512,128]{1,0:T(8,128)}, u32[]{:S(2)}) copy-start(f32[512,128]{1,0:T(8,128)} %copy-done.3) | copy-start | bytes 786436
  66.6 0.9 %copy-start.6 = (f32[31,8,128]{2,1,0:T(8,128)S(1)}, f32[31,8,128]{2,1,0:T(8,128)}, u32[]{:S(2)}) copy-start(f32[31,8,128]{2,1,0:T(8,128)} %copy-done.5) | copy-start | bytes 380932
  67.5 0.7 copy-start.10

commit v5 on v4

--- a/solution.py
+++ b/solution.py
@@ -55,8 +55,9 @@
 
         def speeds(x, best):
             h, m, n = [cells[c, pl.ds(pl.multiple_of(32 * x, 32), 32), :] for c in range(3)]
-            v = jnp.maximum(jnp.abs(m), jnp.abs(n)) / h
-            return jnp.maximum(best, v + jnp.sqrt(h))
+            root = lax.rsqrt(h)
+            v = jnp.maximum(jnp.abs(m), jnp.abs(n)) * (root * root)
+            return jnp.maximum(best, v + h * root)
 
         fastest = lax.fori_loop(chunk * width, (chunk + 1) * width, speeds, fastest, unroll=True)
     for extra in extras:
@@ -138,17 +139,18 @@
 def physical(q, normal):
     h = q[0]
     m = q[normal]
-    v = m / h
+    root = lax.rsqrt(h)
+    v = m * (root * root)
     flux = [m, q[1] * v, q[2] * v, q[3] * v]
     flux[normal] = flux[normal] + 0.5 * h * h
-    return flux, jnp.abs(v) + jnp.sqrt(h)
+    return flux, jnp.abs(v) + h * root
 
 
 def interface(left, right, normal):
     lf, ls = physical(left, normal)
     rf, rs = physical(right, normal)
-    widest = 0.5 * jnp.maximum(ls, rs)
-    return [0.5 * (lf[c] + rf[c]) - widest * (right[c] - left[c]) for c in range(4)]
+    widest = jnp.maximum(ls, rs)
+    return [(lf[c] + rf[c]) - widest * (right[c] - left[c]) for c in range(4)]
 
 
 def inner_kernel(cells, out, lines, fluxes):
@@ -297,7 +299,7 @@
     low = jnp.min(jnp.min(got[...], axis=0, keepdims=True), axis=1, keepdims=True)
     chosen = COURANT * low
     step[...] = chosen
-    ratio = chosen / spacing_of(level[...])
+    ratio = (0.5 * chosen) / spacing_of(level[...])
 
     def border(face, j):
         def part(c, depth):
@@ -409,22 +411,20 @@
     r3 = two_way(jnp.concatenate([ahead(6), beside(5), beside(8), low]), 3)
     r2 = two_way(jnp.concatenate([ahead(4), beside(3), ahead(7), beside(6), low]), 2)
     r1 = two_way(jnp.concatenate([ahead(2), beside(1), ahead(5), beside(4), low]), 1)
-    r4 = two_way(jnp.concatenate([ahead(8), beside(7)]), 4)
     low = jnp.minimum(jnp.minimum(low, r1[4 * T :]), jnp.minimum(r2[4 * T :], r3[3 * T :]))
-    beyond = two_way(low, 4)
+    r4 = two_way(jnp.concatenate([ahead(8), beside(7), low]), 4)
     q = cross(
         jnp.concatenate([ahead(3), beside(2), blk(r1, 2, 2), blk(r2, 2, 2), blk(r3, 2)])
     )
     inside = inner(flat)
     depth = lax.axis_size("patch_2")
     columns = lax.axis_size(("patch_0", "patch_1"))
-    low = jnp.minimum(low, beyond)
+    low = jnp.minimum(low, r4[2 * T :])
     least = jnp.broadcast_to(low[0, :1], (2 * columns, 128))
     groups = [
         [(r * depth + (g + c) % depth) * 2 + c for r in range(columns) for c in range(2)]
         for g in range(depth)
     ]
-    least, r4 = lax.optimization_barrier((least, r4))
     got = lax.all_to_all(least, AXES, 0, 0, tiled=True, axis_index_groups=groups)
     advanced, step = advance(
         flat, inside, rows, deep, r1, r2, r3, r4, w, q, got, level, relation.T, face_half.T,

time: 72.8 us -> 74.9 us (1.029)
  waiting for transfers between devices: 9.2 us -> 17.4 us
  starting transfers between devices: 42 us -> 35.6 us
    ppermute x5 -> x4, waiting for transfers between devices: 4.98 us -> 12.7 us  [two_way(): return lax.ppermute(array, AXES, pairs)]
    ppermute x5 -> x4, starting transfers between devices: 25.1 us -> 18.7 us  [two_way(): return lax.ppermute(array, AXES, pairs)]
  transfers between devices with their start and end apart: 8 -> 7, of which waited for: 3 -> 4; matrix products, arithmetic and copies ran while one was open for 4% -> 3% of each run, Pallas kernels for 5% -> 4%
where the time goes in v5:
time: 74.9 us; the launch traced here: 74.4 us
  starting transfers between devices  35.6 us (48%)
  waiting for transfers between devices  17.4 us (23%)
  local copies, waits for them, and re-layouts  10.6 us (14%)
  Pallas kernels  9.99 us (13%)
  between operations  0.81 us (1%)
    ppermute x4, starting transfers between devices, two_way(): return lax.ppermute(array, AXES, pairs)  18.7 us
    ppermute x4, waiting for transfers between devices, two_way(): return lax.ppermute(array, AXES, pairs)  12.7 us
    ppermute x1, starting transfers between devices, cross(): lax.ppermute(array, AXES, [(i, (i + (-3 if i % 2 else 3)) % n) for i in r...  10.6 us
    unnamed x28, local copies, waits for them, and re-layouts  9.33 us
    all_to_all x1, starting transfers between devices, compute(): lax.all_to_all(least, AXES, 0, 0, tiled=True, axis_index_groups=groups)  4.44 us
    pallas_call x1, Pallas kernels, advance(): pl.pallas_call(step_kernel, out_shape=(jax.ShapeDtypeStruct((4, 1024, 128...  4.29 us
    pallas_call x1, Pallas kernels, inner(): pl.pallas_call(inner_kernel, out_shape=jax.ShapeDtypeStruct((4, 1024, 128...  3.16 us
    all_to_all x1, waiting for transfers between devices, compute(): lax.all_to_all(least, AXES, 0, 0, tiled=True, axis_index_groups=groups)  3.04 us
  transfers between devices with their start and end apart: 7, of which 4 were waited for; matrix products, arithmetic and copies ran while one was open for 3% of the time, Pallas kernels for 4%

profile of v5, /device:TPU:32, one launch (start us, length us, event | category | flops | bytes accessed | tf_op | source)
XLA Modules:
  0.0 74.4 jit_solution(16235062627227802526)
XLA Ops:
  0.6 0.0 copy-start
  0.6 2.5 %pack.1 = (f32[70,8,128]{2,1,0:T(8,128)S(1)}, f32[91,8,128]{2,1,0:T(8,128)S(1)}, f32[1280,128]{1,0:T(8,128)S(1)}, f32[512,128]{1,0:T(8,128)S(1)}) custom-call(f32[4,1024,128]{2,1,0:T(8,128)} %bitcast.15, s32[1,128]{1,0:T(1,128)} %bitcast.21, s32[8,16]{1,0:T(8,128)} %bitcast.23), custom_call_target="tpu_custom_call" | custom-call | tf_op jit(solution)/shard_map/pack/pallas_call | solution.py:117
  3.2 0.0 copy-start.3
  3.2 0.7 copy-done.3
  3.9 1.9 %collective-permute-start = (f32[91,8,128]{2,1,0:T(8,128)S(1)}, f32[91,8,128]{2,1,0:T(8,128)S(1)}, u32[]{:S(2)}, u32[]{:S(2)}) collective-permute-start(f32[91,8,128]{2,1,0:T(8,128)S(1)} %get-tuple-element.11), channel_id=1, source_target_pairs={{0,1},{1,0},{2,3},{3,2},{4,5},{5,4},{6,7},{7,6},{8,9},{9,8},{10,11... | collective-permute-start | bytes 1118216 | tf_op jit(solution)/shard_map/ppermute | solution.py:387
  5.8 1.6 %collective-permute-done.w = f32[91,8,128]{2,1,0:T(8,128)S(1)} collective-permute-done((f32[91,8,128]{2,1,0:T(8,128)S(1)}, f32[91,8,128]{2,1,0:T(8,128)S(1)}, u32[]{:S(2)}, u32[]{:S(2)}) %collective-permute-start) | collective-permute-done | bytes 372768 | tf_op jit(solution)/shard_map/ppermute | solution.py:387
  7.5 0.6 slice_dynamic-update-slice_fusion.8
  8.1 0.6 slice_dynamic-update-slice_fusion.3
  8.7 3.8 %collective-permute-start.1 = (f32[41,8,128]{2,1,0:T(8,128)S(1)}, f32[41,8,128]{2,1,0:T(8,128)S(1)}, u32[]{:S(2)}, u32[]{:S(2)}) collective-permute-start(f32[41,8,128]{2,1,0:T(8,128)S(1)} %constant_dynamic-update-slice_fusion), channel_id=1, source_target_pairs={{0,2},{1,511},{2,4},{3,1},{4,6},{5,3},{6,8},{7,5},{8,10},{9,7},{10... | collective-permute-start | bytes 503816 | tf_op jit(solution)/shard_map/ppermute | solution.py:383
  12.6 6.4 %collective-permute-start.2 = (f32[41,8,128]{2,1,0:T(8,128)S(1)}, f32[41,8,128]{2,1,0:T(8,128)S(1)}, u32[]{:S(2)}, u32[]{:S(2)}) collective-permute-start(f32[41,8,128]{2,1,0:T(8,128)S(1)} %get-tuple-element.14), channel_id=1, source_target_pairs={{0,4},{1,509},{2,6},{3,511},{4,8},{5,1},{6,10},{7,3},{8,12},{9,5},... | collective-permute-start | bytes 503816 | tf_op jit(solution)/shard_map/ppermute | solution.py:383
  19.0 6.5 %collective-permute-start.3 = (f32[31,8,128]{2,1,0:T(8,128)S(1)}, f32[31,8,128]{2,1,0:T(8,128)S(1)}, u32[]{:S(2)}, u32[]{:S(2)}) collective-permute-start(f32[31,8,128]{2,1,0:T(8,128)S(1)} %pad_maximum_fusion), channel_id=1, source_target_pairs={{0,6},{1,507},{2,8},{3,509},{4,10},{5,511},{6,12},{7,1},{8,14},{9,... | collective-permute-start | bytes 380936 | tf_op jit(solution)/shard_map/ppermute | solution.py:383
  25.5 11.4 %collective-permute-done.3.r3 = f32[31,8,128]{2,1,0:T(8,128)S(1)} collective-permute-done((f32[31,8,128]{2,1,0:T(8,128)S(1)}, f32[31,8,128]{2,1,0:T(8,128)S(1)}, u32[]{:S(2)}, u32[]{:S(2)}) %collective-permute-start.3) | collective-permute-done | bytes 127008 | tf_op jit(solution)/shard_map/ppermute | solution.py:383
  36.9 0.0 copy-start.5
  36.9 0.0 collective-permute-done.1.r1
  36.9 0.0 collective-permute-done.2.r2
  36.9 1.9 %collective-permute-start.4 = (f32[21,8,128]{2,1,0:T(8,128)S(1)}, f32[21,8,128]{2,1,0:T(8,128)S(1)}, u32[]{:S(2)}, u32[]{:S(2)}) collective-permute-start(f32[21,8,128]{2,1,0:T(8,128)S(1)} %pad_maximum_fusion.1), channel_id=1, source_target_pairs={{0,8},{1,505},{2,10},{3,507},{4,12},{5,509},{6,14},{7,511},{8,16},... | collective-permute-start | bytes 258056 | tf_op jit(solution)/shard_map/ppermute | solution.py:383
  38.9 0.6 slice_dynamic-update-slice_fusion.1
  39.5 0.6 slice_dynamic-update-slice_fusion
  40.1 0.0 copy-done.5
  40.1 0.6 slice_dynamic-update-slice_fusion.2
  40.8 10.6 %collective-permute-start.5 = (f32[70,8,128]{2,1,0:T(8,128)}, f32[70,8,128]{2,1,0:T(8,128)}, u32[]{:S(2)}, u32[]{:S(2)}) collective-permute-start(f32[70,8,128]{2,1,0:T(8,128)} %slice_dynamic-update-slice_fusion.2), channel_id=1, source_target_pairs={{0,3},{1,510},{2,5},{3,0},{4,7},{5,2},{6,9},{7,4},{8,11},{9,6},{10... | collective-permute-start | bytes 860168 | tf_op jit(solution)/shard_map/ppermute | solution.py:392
  51.3 1.3 %collective-permute-done.4.r4 = f32[21,8,128]{2,1,0:T(8,128)S(1)} collective-permute-done((f32[21,8,128]{2,1,0:T(8,128)S(1)}, f32[21,8,128]{2,1,0:T(8,128)S(1)}, u32[]{:S(2)}, u32[]{:S(2)}) %collective-permute-start.4) | collective-permute-done | bytes 86048 | tf_op jit(solution)/shard_map/ppermute | solution.py:383
  52.7 0.6 broadcast_in_dim.2
  53.3 4.4 %all-to-all-start = ((f32[32,1,128]{2,1,0:T(1,128)}), f32[32,1,128]{2,1,0:T(1,128)}, u32[]{:S(2)}, u32[]{:S(2)}) async-start(f32[32,1,128]{2,1,0:T(1,128)} %broadcast_in_dim.2), calls=%async_computation | async-start | bytes 32768 | tf_op jit(solution)/shard_map/all_to_all | solution.py:428
  57.8 0.0 copy-done
  57.8 0.0 copy-start.7
  57.8 0.0 copy-start.8
  57.8 3.2 %inner.1.inside = f32[4,1024,128]{2,1,0:T(8,128)S(1)} custom-call(f32[4,1024,128]{2,1,0:T(8,128)S(1)} %bitcast.16), custom_call_target="tpu_custom_call" | custom-call | tf_op jit(solution)/shard_map/inner/pallas_call | solution.py:221
  61.0 0.0 copy-start.1
  61.0 1.3 %copy-done.1 = f32[4,1024,128]{2,1,0:T(8,128)} copy-done((f32[4,1024,128]{2,1,0:T(8,128)}, f32[4,1024,128]{2,1,0:T(8,128)S(1)}, u32[]{:S(2)}) %copy-start.1) | copy-done | bytes 2097176
  62.3 3.0 %all-to-all-done = f32[32,1,128]{2,1,0:T(1,128)} async-done(((f32[32,1,128]{2,1,0:T(1,128)}), f32[32,1,128]{2,1,0:T(1,128)}, u32[]{:S(2)}, u32[]{:S(2)}) %all-to-all-start) | async-done | bytes 16416 | tf_op jit(solution)/shard_map/all_to_all | solution.py:428
  65.3 0.0 collective-permute-done.5.q
  65.3 0.0 copy-done.7
  65.3 0.0 copy-done.8
  65.3 0.0 copy-start.2
  65.3 1.6 %copy-done.2 = f32[4,1024,128]{2,1,0:T(8,128)S(1)} copy-done((f32[4,1024,128]{2,1,0:T(8,128)S(1)}, f32[4,1024,128]{2,1,0:T(8,128)}, u32[]{:S(2)}) %copy-start.2) | copy-done | bytes 2097176
  66.9 0.0 copy-start.4
  66.9 0.9 %copy-done.4 = f32[512,128]{1,0:T(8,128)S(1)} copy-done((f32[512,128]{1,0:T(8,128)S(1)}, f32[512,128]{1,0:T(8,128)}, u32[]{:S(2)}) %copy-start.4) | copy-done | bytes 262168
  67.9 0.0 copy-start.6
  67.9 0.9 %copy-done.6 = f32[31,8,128]{2,1,0:T(8,128)S(1)} copy-done((f32[31,8,128]{2,1,0:T(8,128)S(1)}, f32[31,8,128]{2,1,0:T(8,128)}, u32[]{:S(2)}) %copy-start.6) | copy-done | bytes 127000
  68.8 0.0 copy-start.9
  68.8 0.7 copy-done.9
  69.5 0.0 copy-start.10
  69.5 0.7 copy-done.10
  70.1 4.3 %advance.1 = (f32[4,1024,128]{2,1,0:T(8,128)}, f32[1,1]{1,0:T(1,128)}) custom-call(f32[4,1024,128]{2,1,0:T(8,128)S(1)} %bitcast.17, f32[4,1024,128]{2,1,0:T(8,128)S(1)} %copy-done.2, f32[1280,128]{1,0:T(8,128)S(1)} %get-tuple-element.8.rows, f32[512,128]{1,0:T(8,128)S(1)} %copy-done.4, f32[41,8,128]{2,1,0:T(8,128)S(1)} %collective-permute-done.1.r1, ...), custom_call_target="tpu_custom_call" | custom-call | tf_op jit(solution)/shard_map/advance/pallas_call | solution.py:359
  (9 shorter events, 0.1 us)
Async XLA Ops:
  0.6 57.1 %copy-start = (f32[4,32,32,128]{3,2,1,0:T(8,128)S(1)}, f32[4,32,32,128]{3,2,1,0:T(8,128)}, u32[]{:S(2)}) copy-start(f32[4,32,32,128]{3,2,1,0:T(8,128)} %param.6) | copy-start | bytes 6291460
  3.2 0.7 copy-start.3
  3.9 3.6 %collective-permute-start = (f32[91,8,128]{2,1,0:T(8,128)S(1)}, f32[91,8,128]{2,1,0:T(8,128)S(1)}, u32[]{:S(2)}, u32[]{:S(2)}) collective-permute-start(f32[91,8,128]{2,1,0:T(8,128)S(1)} %get-tuple-element.11), channel_id=1, source_target_pairs={{0,1},{1,0},{2,3},{3,2},{4,5},{5,4},{6,7},{7,6},{8,9},{9,8},{10,11... | collective-permute-start | bytes 1118216 | tf_op jit(solution)/shard_map/ppermute | solution.py:387
  8.7 28.2 %collective-permute-start.1 = (f32[41,8,128]{2,1,0:T(8,128)S(1)}, f32[41,8,128]{2,1,0:T(8,128)S(1)}, u32[]{:S(2)}, u32[]{:S(2)}) collective-permute-start(f32[41,8,128]{2,1,0:T(8,128)S(1)} %constant_dynamic-update-slice_fusion), channel_id=1, source_target_pairs={{0,2},{1,511},{2,4},{3,1},{4,6},{5,3},{6,8},{7,5},{8,10},{9,7},{10... | collective-permute-start | bytes 503816 | tf_op jit(solution)/shard_map/ppermute | solution.py:383
  12.6 24.4 %collective-permute-start.2 = (f32[41,8,128]{2,1,0:T(8,128)S(1)}, f32[41,8,128]{2,1,0:T(8,128)S(1)}, u32[]{:S(2)}, u32[]{:S(2)}) collective-permute-start(f32[41,8,128]{2,1,0:T(8,128)S(1)} %get-tuple-element.14), channel_id=1, source_target_pairs={{0,4},{1,509},{2,6},{3,511},{4,8},{5,1},{6,10},{7,3},{8,12},{9,5},... | collective-permute-start | bytes 503816 | tf_op jit(solution)/shard_map/ppermute | solution.py:383
  19.0 17.9 %collective-permute-start.3 = (f32[31,8,128]{2,1,0:T(8,128)S(1)}, f32[31,8,128]{2,1,0:T(8,128)S(1)}, u32[]{:S(2)}, u32[]{:S(2)}) collective-permute-start(f32[31,8,128]{2,1,0:T(8,128)S(1)} %pad_maximum_fusion), channel_id=1, source_target_pairs={{0,6},{1,507},{2,8},{3,509},{4,10},{5,511},{6,12},{7,1},{8,14},{9,... | collective-permute-start | bytes 380936 | tf_op jit(solution)/shard_map/ppermute | solution.py:383
  36.9 3.2 %copy-start.5 = (f32[31,8,128]{2,1,0:T(8,128)}, f32[31,8,128]{2,1,0:T(8,128)S(1)}, u32[]{:S(2)}) copy-start(f32[31,8,128]{2,1,0:T(8,128)S(1)} %collective-permute-done.3.r3) | copy-start | bytes 380932
  36.9 15.7 %collective-permute-start.4 = (f32[21,8,128]{2,1,0:T(8,128)S(1)}, f32[21,8,128]{2,1,0:T(8,128)S(1)}, u32[]{:S(2)}, u32[]{:S(2)}) collective-permute-start(f32[21,8,128]{2,1,0:T(8,128)S(1)} %pad_maximum_fusion.1), channel_id=1, source_target_pairs={{0,8},{1,505},{2,10},{3,507},{4,12},{5,509},{6,14},{7,511},{8,16},... | collective-permute-start | bytes 258056 | tf_op jit(solution)/shard_map/ppermute | solution.py:383
  40.8 24.6 %collective-permute-start.5 = (f32[70,8,128]{2,1,0:T(8,128)}, f32[70,8,128]{2,1,0:T(8,128)}, u32[]{:S(2)}, u32[]{:S(2)}) collective-permute-start(f32[70,8,128]{2,1,0:T(8,128)} %slice_dynamic-update-slice_fusion.2), channel_id=1, source_target_pairs={{0,3},{1,510},{2,5},{3,0},{4,7},{5,2},{6,9},{7,4},{8,11},{9,6},{10... | collective-permute-start | bytes 860168 | tf_op jit(solution)/shard_map/ppermute | solution.py:392
  53.3 12.0 %all-to-all-start = ((f32[32,1,128]{2,1,0:T(1,128)}), f32[32,1,128]{2,1,0:T(1,128)}, u32[]{:S(2)}, u32[]{:S(2)}) async-start(f32[32,1,128]{2,1,0:T(1,128)} %broadcast_in_dim.2), calls=%async_computation | async-start | bytes 32768 | tf_op jit(solution)/shard_map/all_to_all | solution.py:428
  57.8 7.6 %copy-start.7 = (s32[128,4,2]{0,2,1:T(2,128)S(1)}, s32[128,4,2]{0,2,1:T(2,128)}, u32[]{:S(2)}) copy-start(s32[128,4,2]{0,2,1:T(2,128)} %param.10) | copy-start | bytes 12292
  57.8 7.6 %copy-start.8 = (s32[128,4]{0,1:T(4,128)S(1)}, s32[128,4]{0,1:T(4,128)}, u32[]{:S(2)}) copy-start(s32[128,4]{0,1:T(4,128)} %param.8) | copy-start | bytes 6148
  61.0 1.3 %copy-start.1 = (f32[4,1024,128]{2,1,0:T(8,128)}, f32[4,1024,128]{2,1,0:T(8,128)S(1)}, u32[]{:S(2)}) copy-start(f32[4,1024,128]{2,1,0:T(8,128)S(1)} %inner.1.inside) | copy-start | bytes 6291460
  65.3 1.6 %copy-start.2 = (f32[4,1024,128]{2,1,0:T(8,128)S(1)}, f32[4,1024,128]{2,1,0:T(8,128)}, u32[]{:S(2)}) copy-start(f32[4,1024,128]{2,1,0:T(8,128)} %copy-done.1) | copy-start | bytes 6291460
  66.9 0.9 %copy-start.4 = (f32[512,128]{1,0:T(8,128)S(1)}, f32[512,128]{1,0:T(8,128)}, u32[]{:S(2)}) copy-start(f32[512,128]{1,0:T(8,128)} %copy-done.3) | copy-start | bytes 786436
  67.9 0.9 %copy-start.6 = (f32[31,8,128]{2,1,0:T(8,128)S(1)}, f32[31,8,128]{2,1,0:T(8,128)}, u32[]{:S(2)}) copy-start(f32[31,8,128]{2,1,0:T(8,128)} %copy-done.5) | copy-start | bytes 380932
  68.8 0.7 copy-start.9
  69.5 0.7 copy-start.10
